TPU v7x, 32 devices: a whole 2x2x4 slice. The times are simulated.
32 devices in a mesh: data: 2 (over x), outer: 4 (over z), expert: 4 (over y, core).
Axes of the slice: x: 2, y: 2, z: 4, core: 2. Of those that a mesh axis runs over, the one named last changes fastest.
Arguments:
- x_disp: bfloat16 [32, 128, 8, 2048], P('data', ('outer', 'expert')), parts along dimension 0
- w_gate: bfloat16 [128, 2048, 768], P(('outer', 'expert'))
- w_up: bfloat16 [128, 2048, 768], P(('outer', 'expert'))
- w_down: bfloat16 [128, 768, 2048], P(('outer', 'expert'))
- slot_idx: int32 [4096, 8], P(('data', 'outer', 'expert')), parts along dimension 0
- expert_ids: int32 [4096, 8], P(('data', 'outer', 'expert')), parts along dimension 0
- gate_wts: float32 [4096, 8], P(('data', 'outer', 'expert')), parts along dimension 0
Outputs:
- output: bfloat16 [4096, 2048], P(('data', 'outer', 'expert')), parts along dimension 0
There are 2 independent parts. A program takes and returns all parts, laid end to end along the dimension named above; an argument that names none is the same for every part.
All inputs are finite; a program needn't handle non-finite values.
Results may differ from a plain program's by a relative error of at most 0.00824751.
Values are sent between devices in bfloat16 or wider.
A program may use at most 1 GiB of HBM per device.

v0:
```python
import jax
import jax.numpy as jnp
from jax import lax
from jax.sharding import PartitionSpec as P


def expert_rows(x_disp, w_gate, w_up, w_down):
    gate_proj = jnp.einsum("secd,edf->secf", x_disp, w_gate, preferred_element_type=jnp.float32)
    up_proj = jnp.einsum("secd,edf->secf", x_disp, w_up, preferred_element_type=jnp.float32)
    hidden = (jax.nn.silu(gate_proj) * up_proj).astype(jnp.bfloat16)
    return jnp.einsum("secf,efd->secd", hidden, w_down, preferred_element_type=jnp.float32).astype(jnp.bfloat16)


def weighted_sum(y_flat, capacity, slot_idx, expert_ids, gate_wts):
    kept_mask = slot_idx >= 0
    flat_idx = jnp.where(kept_mask, expert_ids * capacity + slot_idx, 0)
    weight = jnp.where(kept_mask, gate_wts, 0.0)
    picked = jnp.take(y_flat, flat_idx, axis=0)
    return jnp.sum(picked.astype(jnp.float32) * weight[:, :, None], axis=1).astype(jnp.bfloat16)


def solution(mesh):
    outer_devs = mesh.shape["outer"]
    inner_devs = mesh.shape["expert"]

    def local_step(x_disp, w_gate, w_up, w_down, slot_idx, expert_ids, gate_wts):
        group_devs, local_experts, capacity, model_width = x_disp.shape
        y_local = expert_rows(x_disp, w_gate, w_up, w_down)
        y_split = y_local.reshape(outer_devs, inner_devs, local_experts, capacity, model_width)
        y_inner = lax.all_to_all(y_split, "expert", 1, 1, tiled=True)
        y_recv = lax.all_to_all(y_inner, "outer", 0, 0, tiled=True)
        y_flat = y_recv.reshape(group_devs * local_experts * capacity, model_width)
        return weighted_sum(y_flat, capacity, slot_idx, expert_ids, gate_wts)

    expert_spec = P(("outer", "expert"))
    token_spec = P(("data", "outer", "expert"))
    return jax.shard_map(local_step, mesh=mesh, in_specs=(P("data", ("outer", "expert")), expert_spec, expert_spec, expert_spec, token_spec, token_spec, token_spec), out_specs=token_spec, check_vma=False)
```

profile of v0, /device:TPU:0, one launch (start us, length us, event | category | flops | bytes accessed | tf_op | source)
XLA Modules:
  0.0 215.4 jit_solution(1964804992229379585)
XLA Ops:
  0.0 13.7 %fusion.2 = f32[8,768,16,8]{1,2,3,0:T(8,128)} fusion(bf16[8,2048,768]{2,1,0:T(8,128)(2,1)} %param.9, bf16[16,8,8,2048]{3,2,1,0:T(8,128)(2,1)} %param.7), kind=kOutput, calls=%fused_computation.3 | convolution fusion | flops 3221225472 | bytes 32505856 | tf_op jit(solution)/shard_map/secd,edf->secf/dot_general | solution.py:9
  13.7 14.4 %fusion.11 = bf16[16,8,8,768]{3,0,2,1:T(8,128)(2,1)S(1)} fusion(f32[8,768,16,8]{1,2,3,0:T(8,128)} %fusion.2, bf16[16,8,8,2048]{3,2,1,0:T(8,128)(2,1)} %param.7, bf16[8,2048,768]{2,1,0:T(8,128)(2,1)} %param.8), kind=kOutput, calls=%fused_computation.13 | convolution fusion | flops 3225944064 | bytes 34078720 | tf_op jit(solution)/shard_map/secd,edf->secf/dot_general | solution.py:8
  28.1 11.8 %fusion.6 = bf16[8,16,8,2048]{3,2,1,0:T(8,128)(2,1)S(1)} fusion(bf16[8,768,2048]{2,1,0:T(8,128)(2,1)} %param.10, bf16[16,8,8,768]{3,0,2,1:T(8,128)(2,1)S(1)} %fusion.11), kind=kOutput, calls=%fused_computation.9 | convolution fusion | flops 3223322624 | bytes 30932992 | tf_op jit(solution)/shard_map/secf,efd->secd/dot_general | solution.py:11
  39.9 0.6 copy.23
  40.5 52.2 %all_to_all.10 = bf16[4,4,8,8,2048]{4,3,0,2,1:T(8,128)(2,1)S(1)} all-to-all(bf16[4,4,8,8,2048]{4,3,0,2,1:T(8,128)(2,1)S(1)} %copy.23), channel_id=1, replica_groups=mesh['data'=2,'outer'=4,'expert'=4] {'expert'}, dimensions={1} | all-to-all | bytes 8388608 | tf_op jit(solution)/shard_map/all_to_all | solution.py:30
  92.8 2.3 %copy.24 = bf16[4,4,8,8,2048]{4,3,1,2,0:T(8,128)(2,1)} copy(bf16[4,4,8,8,2048]{4,3,0,2,1:T(8,128)(2,1)S(1)} %all_to_all.10) | data formatting | bytes 8388608 | tf_op jit(solution)/shard_map/all_to_all | solution.py:30
  95.0 0.0 copy-start
  95.0 0.0 copy-start.2
  95.0 0.0 copy-start.1
  95.0 5.1 %all-to-all-start.1 = ((bf16[4,4,8,8,2048]{4,3,1,2,0:T(8,128)(2,1)}), bf16[4,4,8,8,2048]{4,3,1,2,0:T(8,128)(2,1)}, u32[]{:S(2)}, u32[]{:S(2)}) async-start(bf16[4,4,8,8,2048]{4,3,1,2,0:T(8,128)(2,1)} %copy.24), calls=%async_computation.1 | async-start | bytes 8388608 | tf_op jit(solution)/shard_map/all_to_all | solution.py:31
  100.2 0.0 copy-done
  100.2 0.0 copy-done.2
  100.2 0.1 copy.26
  100.3 0.1 reshape.16
  100.4 0.0 copy-done.1
  100.5 0.1 copy.27
  100.6 0.1 copy.19
  100.7 92.2 %all-to-all-done.1 = bf16[4,4,8,8,2048]{4,3,1,2,0:T(8,128)(2,1)} async-done(((bf16[4,4,8,8,2048]{4,3,1,2,0:T(8,128)(2,1)}), bf16[4,4,8,8,2048]{4,3,1,2,0:T(8,128)(2,1)}, u32[]{:S(2)}, u32[]{:S(2)}) %all-to-all-start.1) | async-done | bytes 4194336 | tf_op jit(solution)/shard_map/all_to_all | solution.py:31
  192.9 4.7 %copy.25 = bf16[4,4,8,8,2048]{4,3,2,1,0:T(8,128)(2,1)} copy(bf16[4,4,8,8,2048]{4,3,1,2,0:T(8,128)(2,1)} %all-to-all-done.1) | data formatting | bytes 8388608 | tf_op jit(solution)/shard_map/all_to_all | solution.py:31
  197.6 11.5 %gather_fusion = bf16[1024,2048]{1,0:T(8,128)(2,1)} fusion(bf16[1024,2048]{1,0:T(8,128)(2,1)} %bitcast.44, s32[1024]{0:T(1024)S(1)} %broadcast_clamp_fusion), kind=kCustom, calls=%fused_computation | custom fusion | bytes 8392704 | tf_op jit(solution)/shard_map/jit(_take)/gather | solution.py:18
  209.2 6.3 %multiply_reduce_fusion = bf16[128,2048]{1,0:T(8,128)(2,1)} fusion(bf16[1024,2048]{1,0:T(8,128)(2,1)} %gather_fusion, f32[128,8]{1,0:T(8,128)S(1)} %copy.27, pred[128,8]{1,0:T(8,128)(4,1)S(1)} %copy.19), kind=kLoop, calls=%fused_computation.7 | loop fusion | flops 8126464 | bytes 4723712 | tf_op jit(solution)/shard_map/reduce_sum | solution.py:19
  (3 shorter events, 0.0 us)
Async XLA Ops:
  95.0 5.2 %copy-start = (s32[128,8]{0,1:T(8,128)S(1)}, s32[128,8]{0,1:T(8,128)}, u32[]{:S(2)}) copy-start(s32[128,8]{0,1:T(8,128)} %param.11) | copy-start | bytes 12292
  95.0 5.2 %copy-start.2 = (s32[128,8]{0,1:T(8,128)S(1)}, s32[128,8]{0,1:T(8,128)}, u32[]{:S(2)}) copy-start(s32[128,8]{0,1:T(8,128)} %param.12) | copy-start | bytes 12292
  95.0 5.4 %copy-start.1 = (f32[128,8]{0,1:T(8,128)S(1)}, f32[128,8]{0,1:T(8,128)}, u32[]{:S(2)}) copy-start(f32[128,8]{0,1:T(8,128)} %param.13) | copy-start | bytes 12292
  95.0 97.8 %all-to-all-start.1 = ((bf16[4,4,8,8,2048]{4,3,1,2,0:T(8,128)(2,1)}), bf16[4,4,8,8,2048]{4,3,1,2,0:T(8,128)(2,1)}, u32[]{:S(2)}, u32[]{:S(2)}) async-start(bf16[4,4,8,8,2048]{4,3,1,2,0:T(8,128)(2,1)} %copy.24), calls=%async_computation.1 | async-start | bytes 8388608 | tf_op jit(solution)/shard_map/all_to_all | solution.py:31
where the time goes:
time: 216 us; the launch traced here: 215 us
  waiting for transfers between devices  92.2 us (43%)
  blocking collectives  52.2 us (24%)
  matrix products  39.9 us (18%)
  local copies, waits for them, and re-layouts  19.6 us (9%)
  other arithmetic  6.3 us (3%)
  starting transfers between devices  5.15 us (2%)
    all_to_all x1, waiting for transfers between devices, local_step(): y_recv = lax.all_to_all(y_inner, 'outer', 0, 0, tiled=True)  92.2 us
    all_to_all x1, blocking collectives, local_step(): y_inner = lax.all_to_all(y_split, 'expert', 1, 1, tiled=True)  52.2 us
    dot_general x1, matrix products, expert_rows(): jnp.einsum('secd,edf->secf', x_disp, w_gate, preferred_element_type=jnp.f...  14.4 us
    dot_general x1, matrix products, expert_rows(): jnp.einsum('secd,edf->secf', x_disp, w_up, preferred_element_type=jnp.flo...  13.7 us
    dot_general x1, matrix products, expert_rows(): jnp.einsum('secf,efd->secd', hidden, w_down, preferred_element_type=jnp.f...  11.8 us
    gather x1, local copies, waits for them, and re-layouts, weighted_sum(): picked = jnp.take(y_flat, flat_idx, axis=0)  11.5 us
    reduce_sum x1, other arithmetic, weighted_sum(): jnp.sum(picked.astype(jnp.float32) * weight[:, :, None], axis=1)  6.28 us
    all_to_all x1, starting transfers between devices, local_step(): y_recv = lax.all_to_all(y_inner, 'outer', 0, 0, tiled=True)  5.15 us
  transfers between devices with their start and end apart: 1, of which 1 were waited for; matrix products, arithmetic and copies ran while one was open for 0% of the time, Pallas kernels for 0%

commit v1 on v0

v1 whole, which is shorter than its diff:
```python
import functools

import jax
import jax.numpy as jnp
from jax import lax
from jax.experimental import pallas as pl
from jax.experimental.pallas import tpu as pltpu
from jax.sharding import PartitionSpec as P

MESH = pl.DeviceIdType.MESH
F32 = jnp.float32
BF16 = jnp.bfloat16
SLOTS = 3
BF16_MAX = 3.3895313892515355e38


def split_columns(width):
    return width // 2, 3 * width // 4


def kernel(outer, inner, x_hbm, wg_hbm, wu_hbm, wd_hbm, slot_ref, ids_ref, gate_ref, out_ref,
           x_buf, wg_buf, wu_buf, wd_buf, h_buf, y_send, y_in, y_out, route_tmp, route_send, route, pick, used,
           part_own, part_send, part_recv, out_buf,
           w_sem, route_ssem, route_rsem, a_ssem, a_rsem, b_ssem, b_rsem, c_ssem, c_rsem, p_ssem, p_rsem, out_sem):
    src, local, cap, width = x_hbm.shape
    tokens, top = slot_ref.shape
    ff = wg_hbm.shape[2]
    rows = src * cap
    span = local * cap
    block = inner * span
    cut_a, cut_b = split_columns(width)
    piece = 256 if width >= 2048 else 128
    o = lax.axis_index("outer")
    i = lax.axis_index("expert")

    def inner_peer(r):
        return lax.rem(i + r, inner)

    def outer_peer(r):
        return lax.rem(o + r, outer)

    def weight_copies(e, slot):
        return (
            pltpu.make_async_copy(x_hbm.at[:, e], x_buf.at[slot], w_sem.at[0, slot]),
            pltpu.make_async_copy(wg_hbm.at[e], wg_buf.at[slot], w_sem.at[1, slot]),
            pltpu.make_async_copy(wu_hbm.at[e], wu_buf.at[slot], w_sem.at[2, slot]),
            pltpu.make_async_copy(wd_hbm.at[e], wd_buf.at[slot], w_sem.at[3, slot]),
        )

    def inner_copy(e, r, lo, hi, ssem, rsem):
        return pltpu.make_async_remote_copy(
            src_ref=y_send.at[e, :, inner_peer(r), :, pl.ds(lo, hi - lo)],
            dst_ref=y_in.at[:, i, e, :, pl.ds(lo, hi - lo)],
            send_sem=ssem.at[e, r - 1], recv_sem=rsem.at[e, r - 1],
            device_id={"expert": inner_peer(r)}, device_id_type=MESH)

    def copy_a(e, r):
        return inner_copy(e, r, 0, cut_a, a_ssem, a_rsem)

    def copy_b(e, r):
        return inner_copy(e, r, cut_a, cut_b, b_ssem, b_rsem)

    def copy_c(e, r):
        return pltpu.make_async_remote_copy(
            src_ref=y_send.at[e, outer_peer(r), :, :, pl.ds(cut_b, width - cut_b)],
            dst_ref=y_out.at[:, o, e],
            send_sem=c_ssem.at[e, r - 1], recv_sem=c_rsem.at[e, r - 1],
            device_id={"outer": outer_peer(r)}, device_id_type=MESH)

    def copy_part(p, r):
        peer = {"outer": outer_peer(r)} if p * piece < cut_b else {"expert": inner_peer(r)}
        return pltpu.make_async_remote_copy(
            src_ref=part_send.at[r - 1, p], dst_ref=part_recv.at[r - 1, p],
            send_sem=p_ssem.at[r - 1, p], recv_sem=p_rsem.at[r - 1, p],
            device_id=peer, device_id_type=MESH)

    def copy_route(q):
        if q < outer - 1:
            r = q + 1
            dst, peer = route.at[o], {"outer": outer_peer(r)}
        else:
            r = q - (outer - 1) + 1
            dst, peer = route.at[outer + i], {"expert": inner_peer(r)}
        return pltpu.make_async_remote_copy(
            src_ref=route_send, dst_ref=dst, send_sem=route_ssem.at[q], recv_sem=route_rsem.at[q],
            device_id=peer, device_id_type=MESH)

    peers = outer + inner - 2
    barrier = pltpu.get_barrier_semaphore()
    for r in range(1, outer):
        pl.semaphore_signal(barrier, inc=1, device_id={"outer": outer_peer(r)}, device_id_type=MESH)
    for r in range(1, inner):
        pl.semaphore_signal(barrier, inc=1, device_id={"expert": inner_peer(r)}, device_id_type=MESH)
    for s in range(SLOTS):
        for c in weight_copies(s, s):
            c.start()

    slot = slot_ref[...]
    flat = jnp.where(slot >= 0, ids_ref[...] * cap + slot, -1).astype(F32)
    route_tmp[...] = jnp.zeros_like(route_tmp)
    route_tmp[:, 0:top] = flat
    route_tmp[:, top:2 * top] = gate_ref[...]
    lanes = route_tmp[...].T[0:2 * top]
    route_send[...] = lanes
    route[o] = lanes
    route[outer + i] = lanes
    pl.semaphore_wait(barrier, peers)
    for q in range(peers):
        copy_route(q).start()
    for q in range(peers):
        copy_route(q).wait_recv()

    row = lax.broadcasted_iota(jnp.int32, (block, tokens), 0)
    row_in = o * block + row
    row_out = (row // span) * block + i * span + row % span

    def build_pick(k):
        want = jnp.where(k < outer, row_in, row_out).astype(F32)
        gates = jnp.zeros((block, tokens), F32)
        hits = jnp.zeros((block, tokens), F32)
        for j in range(top):
            hit = want == route[k, j:j + 1, :]
            gates = jnp.where(hit, route[k, top + j:top + j + 1, :], gates)
            hits = jnp.where(hit, 1.0, hits)
        used[k] = jnp.broadcast_to(jnp.max(hits, axis=1, keepdims=True), (block, tokens)).astype(BF16)
        g = gates.T
        high = jnp.minimum(g, BF16_MAX).astype(BF16)
        rest = g - high.astype(F32)
        mid = rest.astype(BF16)
        low = (rest - mid.astype(F32)).astype(BF16)
        pick[k, 0:tokens] = high
        pick[k, tokens:2 * tokens] = mid
        pick[k, 2 * tokens:3 * tokens] = low

    def expert_step(e, carry):
        s = lax.rem(e, SLOTS)
        copies = weight_copies(e, s)
        build_pick(e)
        copies[0].wait()
        copies[1].wait()
        copies[2].wait()
        x = x_buf[s].reshape(rows, width)
        tile = 256
        for n in range(ff // tile):
            cols = pl.ds(n * tile, tile)
            gate = jnp.dot(x, wg_buf[s, :, cols], preferred_element_type=F32)
            up = jnp.dot(x, wu_buf[s, :, cols], preferred_element_type=F32)
            h_buf[:, cols] = (gate * lax.logistic(gate) * up).astype(BF16)
        copies[3].wait()
        h = h_buf[...]
        for n in range(width // tile):
            cols = pl.ds(n * tile, tile)
            y = jnp.dot(h, wd_buf[s, :, cols], preferred_element_type=F32).astype(BF16)
            y_send[e, :, :, :, cols] = y.reshape(outer, inner, cap, tile)
        y_in[:, i, e] = y_send[e, :, i, :, 0:cut_b]
        y_out[:, o, e] = y_send[e, o, :, :, cut_b:]

        @pl.when(e + SLOTS < local)
        def _():
            for c in weight_copies(e + SLOTS, s):
                c.start()

        for r in range(1, inner):
            copy_a(e, r).start()
        for r in range(1, outer):
            copy_c(e, r).start()
        return carry

    lax.fori_loop(0, local, expert_step, 0)

    def start_b(e, carry):
        for r in range(1, inner):
            copy_b(e, r).start()
        return carry

    lax.fori_loop(0, local, start_b, 0)

    def partial_sum(k, y):
        mask = jnp.concatenate([used[k]] * (piece // tokens), axis=1) > 0
        y = jnp.where(mask, y.reshape(block, piece), jnp.zeros((), BF16))
        s = jnp.dot(pick[k], y, preferred_element_type=F32)
        return s[0:tokens] + s[tokens:2 * tokens] + s[2 * tokens:3 * tokens]

    def combine(p):
        cols = pl.ds(p * piece, piece)
        over_outer = p * piece < cut_b
        n = outer if over_outer else inner
        for r in list(range(1, n)) + [0]:
            if over_outer:
                k = outer_peer(r)
                y = y_in[k, :, :, :, cols]
                total = partial_sum(k, y)
            else:
                k = inner_peer(r)
                y = y_out[k, :, :, :, pl.ds(p * piece - cut_b, piece)]
                total = partial_sum(outer + k, y)
            if r == 0:
                part_own[:, cols] = total
            else:
                part_send[r - 1, p] = total.astype(BF16)
                copy_part(p, r).start()

    def wait_all(copy, n):
        def body(e, carry):
            for r in range(1, n):
                copy(e, r).wait_recv()
            return carry
        lax.fori_loop(0, local, body, 0)

    pieces_a = range(0, cut_a // piece)
    pieces_b = range(cut_a // piece, cut_b // piece)
    pieces_c = range(cut_b // piece, width // piece)
    wait_all(copy_a, inner)
    for p in pieces_a:
        combine(p)
    wait_all(copy_c, outer)
    for p in pieces_c:
        combine(p)
    wait_all(copy_b, inner)
    for p in pieces_b:
        combine(p)

    for p in list(pieces_a) + list(pieces_c) + list(pieces_b):
        cols = pl.ds(p * piece, piece)
        n = outer if p * piece < cut_b else inner
        total = part_own[:, cols]
        for r in range(1, n):
            copy_part(p, r).wait_recv()
            total = total + part_recv[r - 1, p].astype(F32)
        out_buf[:, cols] = total.astype(BF16)

    write = pltpu.make_async_copy(out_buf, out_ref, out_sem)
    write.start()

    for q in range(peers):
        copy_route(q).wait_send()

    def drain(e, carry):
        for r in range(1, inner):
            copy_a(e, r).wait_send()
            copy_b(e, r).wait_send()
        for r in range(1, outer):
            copy_c(e, r).wait_send()
        return carry

    lax.fori_loop(0, local, drain, 0)
    for p in range(width // piece):
        n = outer if p * piece < cut_b else inner
        for r in range(1, n):
            copy_part(p, r).wait_send()
    write.wait()


def solution(mesh):
    outer = mesh.shape["outer"]
    inner = mesh.shape["expert"]

    def local_step(x_disp, w_gate, w_up, w_down, slot_idx, expert_ids, gate_wts):
        src, local, cap, width = x_disp.shape
        tokens, top = slot_idx.shape
        ff = w_gate.shape[2]
        block = inner * local * cap
        sources = outer + inner
        _, cut_b = split_columns(width)
        piece = 256 if width >= 2048 else 128
        dma = pltpu.SemaphoreType.DMA
        anywhere = pl.BlockSpec(memory_space=pl.ANY)
        vmem = pl.BlockSpec(memory_space=pltpu.VMEM)
        return pl.pallas_call(
            functools.partial(kernel, outer, inner),
            out_shape=jax.ShapeDtypeStruct((tokens, width), BF16),
            in_specs=[anywhere] * 4 + [vmem] * 3,
            out_specs=anywhere,
            scratch_shapes=[
                pltpu.VMEM((SLOTS, src, cap, width), BF16),
                pltpu.VMEM((SLOTS, width, ff), BF16),
                pltpu.VMEM((SLOTS, width, ff), BF16),
                pltpu.VMEM((SLOTS, ff, width), BF16),
                pltpu.VMEM((src * cap, ff), BF16),
                pltpu.VMEM((local, outer, inner, cap, width), BF16),
                pltpu.VMEM((outer, inner, local, cap, cut_b), BF16),
                pltpu.VMEM((inner, outer, local, cap, width - cut_b), BF16),
                pltpu.VMEM((tokens, 128), F32),
                pltpu.VMEM((2 * top, tokens), F32),
                pltpu.VMEM((sources, 2 * top, tokens), F32),
                pltpu.VMEM((sources, 3 * tokens, block), BF16),
                pltpu.VMEM((sources, block, tokens), BF16),
                pltpu.VMEM((tokens, width), F32),
                pltpu.VMEM((max(outer, inner) - 1, width // piece, tokens, piece), BF16),
                pltpu.VMEM((max(outer, inner) - 1, width // piece, tokens, piece), BF16),
                pltpu.VMEM((tokens, width), BF16),
                dma((4, SLOTS)),
                dma((outer + inner - 2,)), dma((outer + inner - 2,)),
                dma((local, inner - 1)), dma((local, inner - 1)),
                dma((local, inner - 1)), dma((local, inner - 1)),
                dma((local, outer - 1)), dma((local, outer - 1)),
                dma((max(outer, inner) - 1, width // piece)), dma((max(outer, inner) - 1, width // piece)),
                dma,
            ],
            compiler_params=pltpu.CompilerParams(
                collective_id=0, has_side_effects=True, vmem_limit_bytes=64_000_000),
        )(x_disp, w_gate, w_up, w_down, slot_idx, expert_ids, gate_wts)

    expert_spec = P(("outer", "expert"))
    token_spec = P(("data", "outer", "expert"))
    return jax.shard_map(local_step, mesh=mesh, in_specs=(P("data", ("outer", "expert")), expert_spec, expert_spec, expert_spec, token_spec, token_spec, token_spec), out_specs=token_spec, check_vma=False)
```

time: 216 us -> 80.2 us (0.37)
  waiting for transfers between devices: 92.2 us -> 0 us
  Pallas kernels: 0 us -> 73 us
  blocking collectives: 52.2 us -> 0 us
  matrix products: 39.9 us -> 0 us
  local copies, waits for them, and re-layouts: 19.6 us -> 6.11 us
  other arithmetic: 6.3 us -> 0 us
  starting transfers between devices: 5.15 us -> 0 us
    all_to_all x1 -> x0, waiting for transfers between devices: 92.2 us -> none  [local_step(): y_recv = lax.all_to_all(y_inner, 'outer', 0, 0, tiled=True)]
    pallas_call x0 -> x1, Pallas kernels: none -> 73 us  [local_step(): pl.pallas_call(functools.partial(kernel, outer, inner), out_shape=jax.Sha...]
    all_to_all x1 -> x0, blocking collectives: 52.2 us -> none  [local_step(): y_inner = lax.all_to_all(y_split, 'expert', 1, 1, tiled=True)]
    dot_general x3 -> x0, matrix products: 39.9 us -> none  [the longest x1 14.4 us: expert_rows(): jnp.einsum('secd,edf->secf', x_disp, w_gate, preferred_element_type=jnp.f...]
    gather x1 -> x0, local copies, waits for them, and re-layouts: 11.5 us -> none  [weighted_sum(): picked = jnp.take(y_flat, flat_idx, axis=0)]
    all_to_all x2 -> x0, local copies, waits for them, and re-layouts: 7.02 us -> none  [the longest x1 4.74 us: local_step(): y_recv = lax.all_to_all(y_inner, 'outer', 0, 0, tiled=True)]
    reduce_sum x1 -> x0, other arithmetic: 6.28 us -> none  [weighted_sum(): jnp.sum(picked.astype(jnp.float32) * weight[:, :, None], axis=1)]
    unnamed x6 -> x4, local copies, waits for them, and re-layouts: 0.01 us -> 6.11 us
  transfers between devices with their start and end apart: 1 -> 0, of which waited for: 1 -> 0; matrix products, arithmetic and copies ran while one was open for 0% -> 0% of each run, Pallas kernels for 0% -> 0%
where the time goes in v1:
time: 80.2 us; the launch traced here: 79.1 us
  Pallas kernels  73 us (91%)
  local copies, waits for them, and re-layouts  6.11 us (8%)
    pallas_call x1, Pallas kernels, local_step(): pl.pallas_call(functools.partial(kernel, outer, inner), out_shape=jax.Sha...  73 us
    unnamed x4, local copies, waits for them, and re-layouts  6.11 us

profile of v1, /device:TPU:0, one launch (start us, length us, event | category | flops | bytes accessed | tf_op | source)
XLA Modules:
  0.0 79.1 jit_solution(8522368794837635586)
XLA Ops:
  0.0 1.4 %copy.8.slot_ref = s32[128,8]{1,0:T(8,128)} copy(s32[128,8]{0,1:T(8,128)} %param.11) | data formatting | bytes 8192 | tf_op args[4]
  1.4 1.4 %copy.9.ids_ref = s32[128,8]{1,0:T(8,128)} copy(s32[128,8]{0,1:T(8,128)} %param.12) | data formatting | bytes 8192 | tf_op args[5]
  2.8 1.4 %copy.10.gate_ref = f32[128,8]{1,0:T(8,128)} copy(f32[128,8]{0,1:T(8,128)} %param.13) | data formatting | bytes 8192 | tf_op args[6]
  4.2 73.0 %shard_map.73 = bf16[128,2048]{1,0:T(8,128)(2,1)} custom-call(bf16[16,8,8,2048]{3,2,1,0:T(8,128)(2,1)} %x_hbm.1, bf16[8,2048,768]{2,1,0:T(8,128)(2,1)} %wg_hbm.1, bf16[8,2048,768]{2,1,0:T(8,128)(2,1)} %wu_hbm.1, bf16[8,768,2048]{2,1,0:T(8,128)(2,1)} %wd_hbm.1, s32[128,8]{1,0:T(8,128)} %copy.8.slot_ref, s32[128,8]{1,0:T(8,128)} %copy.9.ids_ref, ...), custom_call_target="tpu_custom_call" | custom-call | tf_op jit(solution)/shard_map/pallas_call | solution.py:269
  77.2 1.9 %copy.12 = bf16[128,2048]{1,0:T(8,128)(2,1)} copy(bf16[128,2048]{1,0:T(8,128)(2,1)} %shard_map.73) | data formatting | bytes 1048576

commit v2 on v1

v2 whole, which is shorter than its diff:
```python
import functools

import jax
import jax.numpy as jnp
from jax import lax
from jax.experimental import pallas as pl
from jax.experimental.pallas import tpu as pltpu
from jax.sharding import PartitionSpec as P

MESH = pl.DeviceIdType.MESH
F32 = jnp.float32
BF16 = jnp.bfloat16
SLOTS = 3
WINDOW = 4
BF16_MAX = 3.3895313892515355e38


def split_columns(width):
    return width // 2, 3 * width // 4


def kernel(outer, inner, x_hbm, wg_hbm, wu_hbm, wd_hbm, slot_ref, ids_ref, gate_ref, out_ref,
           x_buf, wg_buf, wu_buf, wd_buf, h_buf, y_send, y_in, y_out, route_send, route, pick, used,
           own, far, z_send, z_recv, c_send, c_recv, out_buf,
           w_sem, route_ssem, route_rsem, a_ssem, a_rsem, b_ssem, b_rsem, r_ssem, r_rsem,
           z_ssem, z_rsem, c_ssem, c_rsem, out_sem):
    src, local, cap, width = x_hbm.shape
    top, tokens = slot_ref.shape
    ff = wg_hbm.shape[2]
    rows = src * cap
    span = local * cap
    block = inner * span
    cut_a, cut_b = split_columns(width)
    piece = 256 if width >= 2048 else 128
    o = lax.axis_index("outer")
    i = lax.axis_index("expert")
    middle = lax.rem((o + 1) // 2, 2)
    half = o // 2
    near = o + 1 - 2 * lax.rem(o, 2)
    across = (2 - half, 3 - 3 * half)

    def inner_peer(r):
        return lax.rem(i + r, inner)

    def outer_peer(r):
        return lax.rem(o + r, outer)

    def weight_copy(e, kind):
        s = lax.rem(e, SLOTS)
        hbm, buf = ((wg_hbm, wg_buf), (wu_hbm, wu_buf), (wd_hbm, wd_buf))[kind]
        return pltpu.make_async_copy(hbm.at[e], buf.at[s], w_sem.at[kind, s])

    def x_copy(e):
        s = lax.rem(e, SLOTS)
        return pltpu.make_async_copy(x_hbm.at[:, e], x_buf.at[s], w_sem.at[3, s])

    def fetch(e, kind):
        @pl.when(e < local)
        def _():
            if kind == 0:
                x_copy(e).start()
            weight_copy(e, kind).start()

    def inner_copy(e, r, lo, hi, ssem, rsem):
        return pltpu.make_async_remote_copy(
            src_ref=y_send.at[e, :, inner_peer(r), :, pl.ds(lo, hi - lo)],
            dst_ref=y_in.at[:, i, e, :, pl.ds(lo, hi - lo)],
            send_sem=ssem.at[e, r - 1], recv_sem=rsem.at[e, r - 1],
            device_id={"expert": inner_peer(r)}, device_id_type=MESH)

    def copy_a(e, r):
        return inner_copy(e, r, 0, cut_a, a_ssem, a_rsem)

    def copy_b(e, r):
        return inner_copy(e, r, cut_a, cut_b, b_ssem, b_rsem)

    def copy_r(e, r):
        return pltpu.make_async_remote_copy(
            src_ref=y_send.at[e, outer_peer(r), :, :, pl.ds(cut_b, width - cut_b)],
            dst_ref=y_out.at[:, o, e],
            send_sem=r_ssem.at[e, r - 1], recv_sem=r_rsem.at[e, r - 1],
            device_id={"outer": outer_peer(r)}, device_id_type=MESH)

    def copy_z(p, q, slot, peer):
        return pltpu.make_async_remote_copy(
            src_ref=z_send.at[q, p], dst_ref=z_recv.at[slot, p],
            send_sem=z_ssem.at[q, p], recv_sem=z_rsem.at[slot, p],
            device_id={"outer": peer}, device_id_type=MESH)

    def copy_near(p):
        return copy_z(p, 0, 0, near)

    def copy_across(p, k):
        return copy_z(p, 1 + k, middle + (1 - middle) * (2 + k), middle * across[k] + (1 - middle) * near)

    def copy_c(p, r):
        return pltpu.make_async_remote_copy(
            src_ref=c_send.at[r - 1, p], dst_ref=c_recv.at[r - 1, p],
            send_sem=c_ssem.at[r - 1, p], recv_sem=c_rsem.at[r - 1, p],
            device_id={"expert": inner_peer(r)}, device_id_type=MESH)

    def copy_route(q):
        if q < outer - 1:
            r = q + 1
            dst, peer = route.at[o], {"outer": outer_peer(r)}
        else:
            r = q - (outer - 1) + 1
            dst, peer = route.at[outer + i], {"expert": inner_peer(r)}
        return pltpu.make_async_remote_copy(
            src_ref=route_send, dst_ref=dst, send_sem=route_ssem.at[q], recv_sem=route_rsem.at[q],
            device_id=peer, device_id_type=MESH)

    peers = outer + inner - 2
    barrier = pltpu.get_barrier_semaphore()
    for r in range(1, outer):
        pl.semaphore_signal(barrier, inc=1, device_id={"outer": outer_peer(r)}, device_id_type=MESH)
    for r in range(1, inner):
        pl.semaphore_signal(barrier, inc=1, device_id={"expert": inner_peer(r)}, device_id_type=MESH)
    for k in range(WINDOW):
        fetch(k // 3, k % 3)

    slot = slot_ref[...]
    flat = jnp.where(slot >= 0, ids_ref[...] * cap + slot, -1).astype(F32)
    lanes = jnp.concatenate([flat, gate_ref[...]], axis=0)
    route_send[...] = lanes
    route[o] = lanes
    route[outer + i] = lanes
    pl.semaphore_wait(barrier, peers)
    for q in range(peers):
        copy_route(q).start()

    row = lax.broadcasted_iota(jnp.int32, (block, tokens), 0)
    row_in = o * block + row
    row_out = (row // span) * block + i * span + row % span

    def build_pick(k):
        want = jnp.where(k < outer, row_in, row_out).astype(F32)
        gates = jnp.zeros((block, tokens), F32)
        hits = jnp.zeros((block, tokens), F32)
        for j in range(top):
            hit = want == route[k, j:j + 1, :]
            gates = jnp.where(hit, route[k, top + j:top + j + 1, :], gates)
            hits = jnp.where(hit, 1.0, hits)
        used[k] = jnp.broadcast_to(jnp.max(hits, axis=1, keepdims=True), (block, tokens)).astype(BF16)
        g = gates.T
        high = jnp.minimum(g, BF16_MAX).astype(BF16)
        rest = g - high.astype(F32)
        mid = rest.astype(BF16)
        low = (rest - mid.astype(F32)).astype(BF16)
        pick[k, 0:tokens] = high
        pick[k, tokens:2 * tokens] = mid
        pick[k, 2 * tokens:3 * tokens] = low

    def arrived(e, kind):
        if kind == 0:
            x_copy(e).wait()
        weight_copy(e, kind).wait()
        fetch(e + (kind + WINDOW) // 3, (kind + WINDOW) % 3)

    def expert_step(e, carry):
        s = lax.rem(e, SLOTS)
        arrived(e, 0)
        arrived(e, 1)
        x = x_buf[s].reshape(rows, width)
        tile = 256
        for n in range(ff // tile):
            cols = pl.ds(n * tile, tile)
            gate = jnp.dot(x, wg_buf[s, :, cols], preferred_element_type=F32)
            up = jnp.dot(x, wu_buf[s, :, cols], preferred_element_type=F32)
            h_buf[:, cols] = (gate * lax.logistic(gate) * up).astype(BF16)
        arrived(e, 2)
        h = h_buf[...]
        for n in range(width // tile):
            cols = pl.ds(n * tile, tile)
            y = jnp.dot(h, wd_buf[s, :, cols], preferred_element_type=F32).astype(BF16)
            y_send[e, :, :, :, cols] = y.reshape(outer, inner, cap, tile)
        y_in[:, i, e] = y_send[e, :, i, :, 0:cut_b]
        y_out[:, o, e] = y_send[e, o, :, :, cut_b:]
        for r in range(1, inner):
            copy_a(e, r).start()
        for r in range(1, outer):
            copy_r(e, r).start()

        @pl.when(e == 0)
        def _():
            for q in range(peers):
                copy_route(q).wait_recv()

        build_pick(e)
        return carry

    lax.fori_loop(0, local, expert_step, 0)

    def start_b(e, carry):
        for r in range(1, inner):
            copy_b(e, r).start()
        return carry

    lax.fori_loop(0, local, start_b, 0)

    def partial_sum(k, y):
        mask = jnp.concatenate([used[k]] * (piece // tokens), axis=1) > 0
        y = jnp.where(mask, y.reshape(block, piece), jnp.zeros((), BF16))
        s = jnp.dot(pick[k], y, preferred_element_type=F32)
        return s[0:tokens] + s[tokens:2 * tokens] + s[2 * tokens:3 * tokens]

    def columns(p):
        return pl.ds(p * piece, piece)

    def block_sum(p, k):
        return partial_sum(k, y_in[k, :, :, :, columns(p)])

    def wait_all(copy, n):
        def body(e, carry):
            for r in range(1, n):
                copy(e, r).wait_recv()
            return carry
        lax.fori_loop(0, local, body, 0)

    def combine(pieces):
        for p in pieces:
            for k in (1, 0):
                total = block_sum(p, across[k])

                @pl.when(middle == 1)
                def _():
                    far[k, :, columns(p)] = total

                @pl.when(middle == 0)
                def _():
                    z_send[1 + k, p] = total.astype(BF16)
                    copy_across(p, k).start()
        for p in pieces:
            z_send[0, p] = block_sum(p, near).astype(BF16)
            copy_near(p).start()
            own[:, columns(p)] = block_sum(p, o)

    def pass_on(pieces):
        @pl.when(middle == 1)
        def _():
            for p in pieces:
                for k in (1, 0):
                    copy_z(p, 1 + k, 2 + k, near).wait_recv()
                    z_send[1 + k, p] = (far[k, :, columns(p)] + z_recv[2 + k, p].astype(F32)).astype(BF16)
                    copy_across(p, k).start()

    def finish(pieces):
        for p in pieces:
            copy_z(p, 0, 0, near).wait_recv()
            copy_z(p, 1, 1, near).wait_recv()
            out_buf[:, columns(p)] = (own[:, columns(p)] + z_recv[0, p].astype(F32) + z_recv[1, p].astype(F32)).astype(BF16)

    pieces_a = range(0, cut_a // piece)
    pieces_b = range(cut_a // piece, cut_b // piece)
    pieces_c = range((width - cut_b) // piece)
    wait_all(copy_a, inner)
    combine(pieces_a)
    wait_all(copy_r, outer)
    for p in pieces_c:
        for r in range(1, inner):
            k = inner_peer(r)
            c_send[r - 1, p] = partial_sum(outer + k, y_out[k, :, :, :, columns(p)]).astype(BF16)
            copy_c(p, r).start()
        own[:, pl.ds(cut_b + p * piece, piece)] = partial_sum(outer + i, y_out[i, :, :, :, columns(p)])
    pass_on(pieces_a)
    wait_all(copy_b, inner)
    combine(pieces_b)
    pass_on(pieces_b)
    finish(pieces_a)
    for p in pieces_c:
        cols = pl.ds(cut_b + p * piece, piece)
        total = own[:, cols]
        for r in range(1, inner):
            copy_c(p, r).wait_recv()
            total = total + c_recv[r - 1, p].astype(F32)
        out_buf[:, cols] = total.astype(BF16)
    finish(pieces_b)

    write = pltpu.make_async_copy(out_buf, out_ref, out_sem)
    write.start()

    for q in range(peers):
        copy_route(q).wait_send()

    def drain(e, carry):
        for r in range(1, inner):
            copy_a(e, r).wait_send()
            copy_b(e, r).wait_send()
        for r in range(1, outer):
            copy_r(e, r).wait_send()
        return carry

    lax.fori_loop(0, local, drain, 0)
    for p in range(cut_b // piece):
        copy_near(p).wait_send()
        for k in (1, 0):
            copy_across(p, k).wait_send()
    for p in pieces_c:
        for r in range(1, inner):
            copy_c(p, r).wait_send()
    write.wait()


def solution(mesh):
    outer = mesh.shape["outer"]
    inner = mesh.shape["expert"]

    def local_step(x_disp, w_gate, w_up, w_down, slot_idx, expert_ids, gate_wts):
        src, local, cap, width = x_disp.shape
        tokens, top = slot_idx.shape
        ff = w_gate.shape[2]
        block = inner * local * cap
        sources = outer + inner
        _, cut_b = split_columns(width)
        piece = 256 if width >= 2048 else 128
        dma = pltpu.SemaphoreType.DMA
        anywhere = pl.BlockSpec(memory_space=pl.ANY)
        vmem = pl.BlockSpec(memory_space=pltpu.VMEM)
        return pl.pallas_call(
            functools.partial(kernel, outer, inner),
            out_shape=jax.ShapeDtypeStruct((tokens, width), BF16),
            in_specs=[anywhere] * 4 + [vmem] * 3,
            out_specs=anywhere,
            scratch_shapes=[
                pltpu.VMEM((SLOTS, src, cap, width), BF16),
                pltpu.VMEM((SLOTS, width, ff), BF16),
                pltpu.VMEM((SLOTS, width, ff), BF16),
                pltpu.VMEM((SLOTS, ff, width), BF16),
                pltpu.VMEM((src * cap, ff), BF16),
                pltpu.VMEM((local, outer, inner, cap, width), BF16),
                pltpu.VMEM((outer, inner, local, cap, cut_b), BF16),
                pltpu.VMEM((inner, outer, local, cap, width - cut_b), BF16),
                pltpu.VMEM((2 * top, tokens), F32),
                pltpu.VMEM((sources, 2 * top, tokens), F32),
                pltpu.VMEM((sources, 3 * tokens, block), BF16),
                pltpu.VMEM((sources, block, tokens), BF16),
                pltpu.VMEM((tokens, width), F32),
                pltpu.VMEM((2, tokens, cut_b), F32),
                pltpu.VMEM((3, cut_b // piece, tokens, piece), BF16),
                pltpu.VMEM((4, cut_b // piece, tokens, piece), BF16),
                pltpu.VMEM((inner - 1, (width - cut_b) // piece, tokens, piece), BF16),
                pltpu.VMEM((inner - 1, (width - cut_b) // piece, tokens, piece), BF16),
                pltpu.VMEM((tokens, width), BF16),
                dma((4, SLOTS)),
                dma((outer + inner - 2,)), dma((outer + inner - 2,)),
                dma((local, inner - 1)), dma((local, inner - 1)),
                dma((local, inner - 1)), dma((local, inner - 1)),
                dma((local, outer - 1)), dma((local, outer - 1)),
                dma((3, cut_b // piece)), dma((4, cut_b // piece)),
                dma((inner - 1, (width - cut_b) // piece)), dma((inner - 1, (width - cut_b) // piece)),
                dma,
            ],
            compiler_params=pltpu.CompilerParams(
                collective_id=0, has_side_effects=True, vmem_limit_bytes=64_000_000),
        )(x_disp, w_gate, w_up, w_down, slot_idx.T, expert_ids.T, gate_wts.T)

    expert_spec = P(("outer", "expert"))
    token_spec = P(("data", "outer", "expert"))
    return jax.shard_map(local_step, mesh=mesh, in_specs=(P("data", ("outer", "expert")), expert_spec, expert_spec, expert_spec, token_spec, token_spec, token_spec), out_specs=token_spec, check_vma=False)
```

time: 80.2 us -> 65.5 us (0.82)
  Pallas kernels: 73 us -> 63 us
  local copies, waits for them, and re-layouts: 6.11 us -> 1.88 us
    pallas_call x1, Pallas kernels: 73 us -> 63 us  [local_step(): pl.pallas_call(functools.partial(kernel, outer, inner), out_shape=jax.Sha...]
    unnamed x4 -> x1, local copies, waits for them, and re-layouts: 6.11 us -> 1.88 us
where the time goes in v2:
time: 65.5 us; the launch traced here: 64.9 us
  Pallas kernels  63 us (96%)
  local copies, waits for them, and re-layouts  1.88 us (3%)
    pallas_call x1, Pallas kernels, local_step(): pl.pallas_call(functools.partial(kernel, outer, inner), out_shape=jax.Sha...  63 us
    unnamed x1, local copies, waits for them, and re-layouts  1.88 us

profile of v2, /device:TPU:0, one launch (start us, length us, event | category | flops | bytes accessed | tf_op | source)
XLA Modules:
  0.0 64.9 jit_solution(3109744201291058755)
XLA Ops:
  0.0 63.0 %shard_map.73 = bf16[128,2048]{1,0:T(8,128)(2,1)} custom-call(bf16[16,8,8,2048]{3,2,1,0:T(8,128)(2,1)} %x_hbm.1, bf16[8,2048,768]{2,1,0:T(8,128)(2,1)} %wg_hbm.1, bf16[8,2048,768]{2,1,0:T(8,128)(2,1)} %wu_hbm.1, bf16[8,768,2048]{2,1,0:T(8,128)(2,1)} %wd_hbm.1, s32[8,128]{1,0:T(8,128)} %bitcast.3, s32[8,128]{1,0:T(8,128)} %bitcast.4, f32[8,128]{1,0:T(8,128)} %bitcast.5), custom_call_target="tpu_custom_call" | custom-call | tf_op jit(solution)/shard_map/pallas_call | solution.py:319
  63.0 1.9 %copy.9 = bf16[128,2048]{1,0:T(8,128)(2,1)} copy(bf16[128,2048]{1,0:T(8,128)(2,1)} %shard_map.73) | data formatting | bytes 1048576

commit v3 on v2

v3 whole, which is shorter than its diff:
```python
import functools

import jax
import jax.numpy as jnp
from jax import lax
from jax.experimental import pallas as pl
from jax.experimental.pallas import tpu as pltpu
from jax.sharding import PartitionSpec as P

MESH = pl.DeviceIdType.MESH
F32 = jnp.float32
BF16 = jnp.bfloat16
SLOTS = 3
WINDOW = 4
BF16_MAX = 3.3895313892515355e38


def column_plan(width):
    unit = width // 8
    return unit, (0, 2 * unit, 4 * unit, 6 * unit)


def kernel(outer, inner, x_hbm, wg_hbm, wu_hbm, wd_hbm, slot_ref, ids_ref, gate_ref, out_ref,
           x_buf, wg_buf, wu_buf, wd_buf, h_buf, y_send, y_in, y_out, route_send, route, pick, used,
           own, far, z_send, z_recv, c_send, c_recv,
           w_sem, route_ssem, route_rsem, i_ssem, i_rsem, r_ssem, r_rsem, z_ssem, z_rsem, c_ssem, c_rsem):
    src, local, cap, width = x_hbm.shape
    top, tokens = slot_ref.shape
    ff = wg_hbm.shape[2]
    rows = src * cap
    span = local * cap
    block = inner * span
    piece, bounds = column_plan(width)
    chunks = len(bounds) - 1
    split = bounds[-1]
    o = lax.axis_index("outer")
    i = lax.axis_index("expert")
    middle = lax.rem((o + 1) // 2, 2)
    half = o // 2
    near = o + 1 - 2 * lax.rem(o, 2)
    across = (2 - half, 3 - 3 * half)

    def inner_peer(r):
        return lax.rem(i + r, inner)

    def outer_peer(r):
        return lax.rem(o + r, outer)

    def weight_copy(e, kind):
        s = lax.rem(e, SLOTS)
        hbm, buf = ((wg_hbm, wg_buf), (wu_hbm, wu_buf), (wd_hbm, wd_buf))[kind]
        return pltpu.make_async_copy(hbm.at[e], buf.at[s], w_sem.at[kind, s])

    def x_copy(e):
        s = lax.rem(e, SLOTS)
        return pltpu.make_async_copy(x_hbm.at[:, e], x_buf.at[s], w_sem.at[3, s])

    def fetch(e, kind):
        @pl.when(e < local)
        def _():
            if kind == 0:
                x_copy(e).start()
            weight_copy(e, kind).start()

    def arrived(e, kind):
        if kind == 0:
            x_copy(e).wait()
        weight_copy(e, kind).wait()
        fetch(e + (kind + WINDOW) // 3, (kind + WINDOW) % 3)

    def inner_copy(src_ref, dst_ref, n, r):
        return pltpu.make_async_remote_copy(
            src_ref=src_ref, dst_ref=dst_ref, send_sem=i_ssem.at[n, r - 1], recv_sem=i_rsem.at[n, r - 1],
            device_id={"expert": inner_peer(r)}, device_id_type=MESH)

    def chunk_cols(n):
        return pl.ds(bounds[n], bounds[n + 1] - bounds[n])

    def send_inner(e, n):
        for r in range(1, inner):
            inner_copy(y_send.at[e, :, inner_peer(r), :, chunk_cols(n)], y_in.at[:, i, e, :, chunk_cols(n)], n, r).start()

    def all_inner(n, r):
        return inner_copy(y_send.at[:, :, inner_peer(r), :, chunk_cols(n)],
                          y_in.at[:, lax.rem(i + inner - r, inner), :, :, chunk_cols(n)], n, r)

    def outer_copy(src_ref, dst_ref, r):
        return pltpu.make_async_remote_copy(
            src_ref=src_ref, dst_ref=dst_ref, send_sem=r_ssem.at[r - 1], recv_sem=r_rsem.at[r - 1],
            device_id={"outer": outer_peer(r)}, device_id_type=MESH)

    rest_cols = pl.ds(split, width - split)

    def send_outer(e):
        for r in range(1, outer):
            outer_copy(y_send.at[e, outer_peer(r), :, :, rest_cols], y_out.at[:, o, e], r).start()

    def all_outer(r):
        return outer_copy(y_send.at[:, outer_peer(r), :, :, rest_cols], y_out.at[:, lax.rem(o + outer - r, outer)], r)

    def copy_z(p, q, slot, peer):
        return pltpu.make_async_remote_copy(
            src_ref=z_send.at[q, p], dst_ref=z_recv.at[slot, p],
            send_sem=z_ssem.at[q, p], recv_sem=z_rsem.at[slot, p],
            device_id={"outer": peer}, device_id_type=MESH)

    def copy_near(p):
        return copy_z(p, 0, 0, near)

    def copy_across(p, k):
        return copy_z(p, 1 + k, middle + (1 - middle) * (2 + k), middle * across[k] + (1 - middle) * near)

    def copy_c(p, r):
        return pltpu.make_async_remote_copy(
            src_ref=c_send.at[r - 1, p], dst_ref=c_recv.at[r - 1, p],
            send_sem=c_ssem.at[r - 1, p], recv_sem=c_rsem.at[r - 1, p],
            device_id={"expert": inner_peer(r)}, device_id_type=MESH)

    def copy_route(q):
        if q < outer - 1:
            dst, peer = route.at[o], {"outer": outer_peer(q + 1)}
        else:
            dst, peer = route.at[outer + i], {"expert": inner_peer(q - outer + 2)}
        return pltpu.make_async_remote_copy(
            src_ref=route_send, dst_ref=dst, send_sem=route_ssem.at[q], recv_sem=route_rsem.at[q],
            device_id=peer, device_id_type=MESH)

    for k in range(WINDOW):
        fetch(k // 3, k % 3)
    peers = outer + inner - 2
    barrier = pltpu.get_barrier_semaphore()
    for r in range(1, outer):
        pl.semaphore_signal(barrier, inc=1, device_id={"outer": outer_peer(r)}, device_id_type=MESH)
    for r in range(1, inner):
        pl.semaphore_signal(barrier, inc=1, device_id={"expert": inner_peer(r)}, device_id_type=MESH)

    slot = slot_ref[...]
    flat = jnp.where(slot >= 0, ids_ref[...] * cap + slot, -1).astype(F32)
    lanes = jnp.concatenate([flat, gate_ref[...]], axis=0)
    route_send[...] = lanes
    route[o] = lanes
    route[outer + i] = lanes
    pl.semaphore_wait(barrier, peers)
    for q in range(peers):
        copy_route(q).start()

    row = lax.broadcasted_iota(jnp.int32, (block, tokens), 0)
    row_in = o * block + row
    row_out = (row // span) * block + i * span + row % span

    def build_pick(k):
        want = jnp.where(k < outer, row_in, row_out).astype(F32)
        gates = jnp.zeros((block, tokens), F32)
        hits = jnp.zeros((block, tokens), F32)
        for j in range(top):
            hit = want == route[k, j:j + 1, :]
            gates = jnp.where(hit, route[k, top + j:top + j + 1, :], gates)
            hits = jnp.where(hit, 1.0, hits)
        used[k] = jnp.broadcast_to(jnp.max(hits, axis=1, keepdims=True), (block, tokens)).astype(BF16)
        g = gates.T
        high = jnp.minimum(g, BF16_MAX).astype(BF16)
        rest = g - high.astype(F32)
        mid = rest.astype(BF16)
        low = (rest - mid.astype(F32)).astype(BF16)
        pick[k, 0:tokens] = high
        pick[k, tokens:2 * tokens] = mid
        pick[k, 2 * tokens:3 * tokens] = low

    def expert_step(e, carry):
        s = lax.rem(e, SLOTS)
        arrived(e, 0)
        arrived(e, 1)
        x = x_buf[s].reshape(rows, width)
        tile = 256
        for n in range(ff // tile):
            cols = pl.ds(n * tile, tile)
            gate = jnp.dot(x, wg_buf[s, :, cols], preferred_element_type=F32)
            up = jnp.dot(x, wu_buf[s, :, cols], preferred_element_type=F32)
            h_buf[:, cols] = (gate * lax.logistic(gate) * up).astype(BF16)
        arrived(e, 2)
        h = h_buf[...]

        def down(lo, hi):
            for c in range(lo, hi, piece):
                cols = pl.ds(c, piece)
                y = jnp.dot(h, wd_buf[s, :, cols], preferred_element_type=F32).astype(BF16)
                y_send[e, :, :, :, cols] = y.reshape(outer, inner, cap, piece)

        down(bounds[0], bounds[1])
        down(split, width)
        send_inner(e, 0)
        down(bounds[1], bounds[2])
        send_outer(e)
        down(bounds[2], split)
        send_inner(e, 1)
        y_in[:, i, e] = y_send[e, :, i, :, 0:split]
        y_out[:, o, e] = y_send[e, o, :, :, split:]

        @pl.when(e == 0)
        def _():
            for q in range(peers):
                copy_route(q).wait_recv()

        build_pick(e)
        return carry

    lax.fori_loop(0, local, expert_step, 0)

    def send_last(e, carry):
        send_inner(e, 2)
        return carry

    lax.fori_loop(0, local, send_last, 0)

    def partial_sum(k, y):
        mask = jnp.concatenate([used[k]] * (piece // tokens), axis=1) > 0
        y = jnp.where(mask, y.reshape(block, piece), jnp.zeros((), BF16))
        s = jnp.dot(pick[k], y, preferred_element_type=F32)
        return s[0:tokens] + s[tokens:2 * tokens] + s[2 * tokens:3 * tokens]

    def columns(p):
        return pl.ds(p * piece, piece)

    def block_sum(p, k):
        return partial_sum(k, y_in[k, :, :, :, columns(p)])

    def pieces_of(n):
        return range(bounds[n] // piece, bounds[n + 1] // piece)

    def combine(n):
        for r in range(1, inner):
            all_inner(n, r).wait_recv()
        for p in pieces_of(n):
            for k in (1, 0):
                total = block_sum(p, across[k])

                @pl.when(middle == 1)
                def _():
                    far[k, :, columns(p)] = total

                @pl.when(middle == 0)
                def _():
                    z_send[1 + k, p] = total.astype(BF16)
                    copy_across(p, k).start()
        for p in pieces_of(n):
            z_send[0, p] = block_sum(p, near).astype(BF16)
            copy_near(p).start()
        for p in pieces_of(n):
            own[:, columns(p)] = block_sum(p, o)

    def pass_on(n):
        @pl.when(middle == 1)
        def _():
            for p in pieces_of(n):
                for k in (1, 0):
                    copy_z(p, 1 + k, 2 + k, near).wait_recv()
                    z_send[1 + k, p] = (far[k, :, columns(p)] + z_recv[2 + k, p].astype(F32)).astype(BF16)
                    copy_across(p, k).start()

    def finish(n):
        for p in pieces_of(n):
            copy_z(p, 0, 0, near).wait_recv()
            copy_z(p, 1, 1, near).wait_recv()
            out_ref[:, columns(p)] = (own[:, columns(p)] + z_recv[0, p].astype(F32) + z_recv[1, p].astype(F32)).astype(BF16)

    rest_pieces = range((width - split) // piece)
    combine(0)
    combine(1)
    for r in range(1, outer):
        all_outer(r).wait_recv()
    for p in rest_pieces:
        for r in range(1, inner):
            k = inner_peer(r)
            c_send[r - 1, p] = partial_sum(outer + k, y_out[k, :, :, :, columns(p)]).astype(BF16)
            copy_c(p, r).start()
        own[:, pl.ds(split + p * piece, piece)] = partial_sum(outer + i, y_out[i, :, :, :, columns(p)])
    pass_on(0)
    pass_on(1)
    combine(2)
    pass_on(2)
    finish(0)
    finish(1)
    for p in rest_pieces:
        cols = pl.ds(split + p * piece, piece)
        total = own[:, cols]
        for r in range(1, inner):
            copy_c(p, r).wait_recv()
            total = total + c_recv[r - 1, p].astype(F32)
        out_ref[:, cols] = total.astype(BF16)

    for q in range(peers):
        copy_route(q).wait_send()
    for r in range(1, inner):
        for n in range(chunks):
            all_inner(n, r).wait_send()
        for p in rest_pieces:
            copy_c(p, r).wait_send()
    for r in range(1, outer):
        all_outer(r).wait_send()
    for p in range(split // piece):
        copy_near(p).wait_send()
        for k in (1, 0):
            copy_across(p, k).wait_send()
    finish(2)


def solution(mesh):
    outer = mesh.shape["outer"]
    inner = mesh.shape["expert"]

    def local_step(x_disp, w_gate, w_up, w_down, slot_idx, expert_ids, gate_wts):
        src, local, cap, width = x_disp.shape
        tokens, top = slot_idx.shape
        ff = w_gate.shape[2]
        block = inner * local * cap
        sources = outer + inner
        piece, bounds = column_plan(width)
        chunks = len(bounds) - 1
        split = bounds[-1]
        peers = outer + inner - 2
        dma = pltpu.SemaphoreType.DMA
        anywhere = pl.BlockSpec(memory_space=pl.ANY)
        vmem = pl.BlockSpec(memory_space=pltpu.VMEM)
        return pl.pallas_call(
            functools.partial(kernel, outer, inner),
            out_shape=jax.ShapeDtypeStruct((tokens, width), BF16),
            in_specs=[anywhere] * 4 + [vmem] * 3,
            out_specs=vmem,
            scratch_shapes=[
                pltpu.VMEM((SLOTS, src, cap, width), BF16),
                pltpu.VMEM((SLOTS, width, ff), BF16),
                pltpu.VMEM((SLOTS, width, ff), BF16),
                pltpu.VMEM((SLOTS, ff, width), BF16),
                pltpu.VMEM((src * cap, ff), BF16),
                pltpu.VMEM((local, outer, inner, cap, width), BF16),
                pltpu.VMEM((outer, inner, local, cap, split), BF16),
                pltpu.VMEM((inner, outer, local, cap, width - split), BF16),
                pltpu.VMEM((2 * top, tokens), F32),
                pltpu.VMEM((sources, 2 * top, tokens), F32),
                pltpu.VMEM((sources, 3 * tokens, block), BF16),
                pltpu.VMEM((sources, block, tokens), BF16),
                pltpu.VMEM((tokens, width), F32),
                pltpu.VMEM((2, tokens, split), F32),
                pltpu.VMEM((3, split // piece, tokens, piece), BF16),
                pltpu.VMEM((4, split // piece, tokens, piece), BF16),
                pltpu.VMEM((inner - 1, (width - split) // piece, tokens, piece), BF16),
                pltpu.VMEM((inner - 1, (width - split) // piece, tokens, piece), BF16),
                dma((4, SLOTS)),
                dma((peers,)), dma((peers,)),
                dma((chunks, inner - 1)), dma((chunks, inner - 1)),
                dma((outer - 1,)), dma((outer - 1,)),
                dma((3, split // piece)), dma((4, split // piece)),
                dma((inner - 1, (width - split) // piece)), dma((inner - 1, (width - split) // piece)),
            ],
            compiler_params=pltpu.CompilerParams(
                collective_id=0, has_side_effects=True, vmem_limit_bytes=54_000_000),
        )(x_disp, w_gate, w_up, w_down, slot_idx.T, expert_ids.T, gate_wts.T)

    expert_spec = P(("outer", "expert"))
    token_spec = P(("data", "outer", "expert"))
    return jax.shard_map(local_step, mesh=mesh, in_specs=(P("data", ("outer", "expert")), expert_spec, expert_spec, expert_spec, token_spec, token_spec, token_spec), out_specs=token_spec, check_vma=False)
```

time: 65.5 us -> 63.7 us (0.973)
  Pallas kernels: 63 us -> 60.6 us
  local copies, waits for them, and re-layouts: 1.88 us -> 2.85 us
    pallas_call x1, Pallas kernels: 63 us -> 60.6 us  [local_step(): pl.pallas_call(functools.partial(kernel, outer, inner), out_shape=jax.Sha...]
    unnamed x1 -> x7, local copies, waits for them, and re-layouts: 1.88 us -> 2.85 us
where the time goes in v3:
time: 63.7 us; the launch traced here: 63.5 us
  Pallas kernels  60.6 us (95%)
  local copies, waits for them, and re-layouts  2.85 us (4%)
    pallas_call x1, Pallas kernels, local_step(): pl.pallas_call(functools.partial(kernel, outer, inner), out_shape=jax.Sha...  60.6 us
    unnamed x7, local copies, waits for them, and re-layouts  2.85 us

profile of v3, /device:TPU:0, one launch (start us, length us, event | category | flops | bytes accessed | tf_op | source)
XLA Modules:
  0.0 63.5 jit_solution(15711068219226410543)
XLA Ops:
  0.0 0.0 copy-start
  0.0 0.7 %copy-done = s32[128,8]{0,1:T(8,128)S(1)} copy-done((s32[128,8]{0,1:T(8,128)S(1)}, s32[128,8]{0,1:T(8,128)}, u32[]{:S(2)}) %copy-start) | copy-done | bytes 4120
  0.7 0.0 copy-start.1
  0.7 0.7 %copy-done.1 = s32[128,8]{0,1:T(8,128)S(1)} copy-done((s32[128,8]{0,1:T(8,128)S(1)}, s32[128,8]{0,1:T(8,128)}, u32[]{:S(2)}) %copy-start.1) | copy-done | bytes 4120
  1.4 0.0 copy-start.2
  1.4 0.7 %copy-done.2 = f32[128,8]{0,1:T(8,128)S(1)} copy-done((f32[128,8]{0,1:T(8,128)S(1)}, f32[128,8]{0,1:T(8,128)}, u32[]{:S(2)}) %copy-start.2) | copy-done | bytes 4120
  2.1 60.6 %shard_map.73 = bf16[128,2048]{1,0:T(8,128)(2,1)S(1)} custom-call(bf16[16,8,8,2048]{3,2,1,0:T(8,128)(2,1)} %x_hbm.1, bf16[8,2048,768]{2,1,0:T(8,128)(2,1)} %wg_hbm.1, bf16[8,2048,768]{2,1,0:T(8,128)(2,1)} %wu_hbm.1, bf16[8,768,2048]{2,1,0:T(8,128)(2,1)} %wd_hbm.1, s32[8,128]{1,0:T(8,128)S(1)} %bitcast.3, s32[8,128]{1,0:T(8,128)S(1)} %bitcast.4, ...), custom_call_target="tpu_custom_call" | custom-call | tf_op jit(solution)/shard_map/pallas_call | solution.py:324
  62.7 0.8 %copy.9 = bf16[128,2048]{1,0:T(8,128)(2,1)} copy(bf16[128,2048]{1,0:T(8,128)(2,1)S(1)} %shard_map.73) | data formatting | bytes 1048576
Async XLA Ops:
  0.0 0.7 %copy-start = (s32[128,8]{0,1:T(8,128)S(1)}, s32[128,8]{0,1:T(8,128)}, u32[]{:S(2)}) copy-start(s32[128,8]{0,1:T(8,128)} %param.11) | copy-start | bytes 12292
  0.7 0.7 %copy-start.1 = (s32[128,8]{0,1:T(8,128)S(1)}, s32[128,8]{0,1:T(8,128)}, u32[]{:S(2)}) copy-start(s32[128,8]{0,1:T(8,128)} %param.12) | copy-start | bytes 12292
  1.4 0.7 %copy-start.2 = (f32[128,8]{0,1:T(8,128)S(1)}, f32[128,8]{0,1:T(8,128)}, u32[]{:S(2)}) copy-start(f32[128,8]{0,1:T(8,128)} %param.13) | copy-start | bytes 12292

commit v4 on v3

v4 whole, which is shorter than its diff:
```python
import functools

import jax
import jax.numpy as jnp
from jax import lax
from jax.experimental import pallas as pl
from jax.experimental.pallas import tpu as pltpu
from jax.sharding import PartitionSpec as P

MESH = pl.DeviceIdType.MESH
F32 = jnp.float32
BF16 = jnp.bfloat16
SLOTS = 3
WINDOW = 4
BF16_MAX = 3.3895313892515355e38


CHUNKS = 8
FIRST = (0, 1, 2)
LATER = 3
MIXED = (4, 5)
OUTER = (6, 7)
INNER_CHUNKS = 6


def kernel(outer, inner, x_hbm, wg_hbm, wu_hbm, wd_hbm, slot_hbm, ids_hbm, gate_hbm, out_ref,
           x_buf, wg_buf, wu_buf, wd_buf, h_buf, y_send, y_in, y_out, y_half, slot_ref, ids_ref, gate_ref, route_send, route, pick, used,
           own, far, z_send, z_recv, c_send, c_recv,
           w_sem, t_sem, route_ssem, route_rsem, i_ssem, i_rsem, r_ssem, r_rsem, h_ssem, h_rsem, z_ssem, z_rsem, c_ssem, c_rsem):
    src, local, cap, width = x_hbm.shape
    top, tokens = slot_hbm.shape
    ff = wg_hbm.shape[2]
    rows = src * cap
    span = local * cap
    block = inner * span
    piece = width // CHUNKS
    split = INNER_CHUNKS * piece
    mixed = MIXED[0] * piece
    o = lax.axis_index("outer")
    i = lax.axis_index("expert")
    middle = lax.rem((o + 1) // 2, 2)
    half = o // 2
    seat = lax.rem(o, 2)
    near = o + 1 - 2 * seat
    across = (2 - half, 3 - 3 * half)

    def inner_peer(r):
        return lax.rem(i + r, inner)

    def outer_peer(r):
        return lax.rem(o + r, outer)

    def weight_copy(e, kind):
        s = lax.rem(e, SLOTS)
        hbm, buf = ((wg_hbm, wg_buf), (wu_hbm, wu_buf), (wd_hbm, wd_buf))[kind]
        return pltpu.make_async_copy(hbm.at[e], buf.at[s], w_sem.at[kind, s])

    def x_copy(e):
        s = lax.rem(e, SLOTS)
        return pltpu.make_async_copy(x_hbm.at[:, e], x_buf.at[s], w_sem.at[3, s])

    def fetch(e, kind):
        @pl.when(e < local)
        def _():
            if kind == 0:
                x_copy(e).start()
            weight_copy(e, kind).start()

    def arrived(e, kind):
        if kind == 0:
            x_copy(e).wait()
        weight_copy(e, kind).wait()
        fetch(e + (kind + WINDOW) // 3, (kind + WINDOW) % 3)

    def inner_copy(src_ref, dst_ref, n, r):
        return pltpu.make_async_remote_copy(
            src_ref=src_ref, dst_ref=dst_ref, send_sem=i_ssem.at[n, r - 1], recv_sem=i_rsem.at[n, r - 1],
            device_id={"expert": inner_peer(r)}, device_id_type=MESH)

    def chunk_cols(n):
        return pl.ds(n * piece, piece)

    def blocks(n):
        return pl.ds(2 * (1 - half), 2) if n in MIXED else pl.ds(0, outer)

    def send_inner(e, n):
        for r in range(1, inner):
            inner_copy(y_send.at[e, blocks(n), inner_peer(r), :, chunk_cols(n)],
                       y_in.at[blocks(n), i, e, :, chunk_cols(n)], n, r).start()

    def all_inner(n, r):
        return inner_copy(y_send.at[:, blocks(n), inner_peer(r), :, chunk_cols(n)],
                          y_in.at[blocks(n), lax.rem(i + inner - r, inner), :, :, chunk_cols(n)], n, r)

    def outer_copy(src_ref, dst_ref, r):
        return pltpu.make_async_remote_copy(
            src_ref=src_ref, dst_ref=dst_ref, send_sem=r_ssem.at[r - 1], recv_sem=r_rsem.at[r - 1],
            device_id={"outer": outer_peer(r)}, device_id_type=MESH)

    rest_cols = pl.ds(split, width - split)

    def send_outer(e):
        for r in range(1, outer):
            outer_copy(y_send.at[e, outer_peer(r), :, :, rest_cols], y_out.at[:, o, e], r).start()

    def all_outer(r):
        return outer_copy(y_send.at[:, outer_peer(r), :, :, rest_cols], y_out.at[:, lax.rem(o + outer - r, outer)], r)

    half_cols = pl.ds(mixed, split - mixed)

    def half_copy(src_ref, dst_ref):
        return pltpu.make_async_remote_copy(
            src_ref=src_ref, dst_ref=dst_ref, send_sem=h_ssem, recv_sem=h_rsem,
            device_id={"outer": near}, device_id_type=MESH)

    def send_half(e):
        half_copy(y_send.at[e, near, :, :, half_cols], y_half.at[:, seat, e]).start()

    def all_half():
        return half_copy(y_send.at[:, near, :, :, half_cols], y_half.at[:, 1 - seat])

    def copy_z(p, q, slot, peer):
        return pltpu.make_async_remote_copy(
            src_ref=z_send.at[q, p], dst_ref=z_recv.at[slot, p],
            send_sem=z_ssem.at[q, p], recv_sem=z_rsem.at[slot, p],
            device_id={"outer": peer}, device_id_type=MESH)

    def copy_near(p):
        return copy_z(p, 0, 0, near)

    def copy_across(p, k):
        return copy_z(p, 1 + k, middle + (1 - middle) * (2 + k), middle * across[k] + (1 - middle) * near)

    def copy_c(p, r):
        return pltpu.make_async_remote_copy(
            src_ref=c_send.at[r - 1, p], dst_ref=c_recv.at[r - 1, p],
            send_sem=c_ssem.at[r - 1, p], recv_sem=c_rsem.at[r - 1, p],
            device_id={"expert": inner_peer(r)}, device_id_type=MESH)

    def copy_route(q):
        if q < outer - 1:
            dst, peer = route.at[o], {"outer": outer_peer(q + 1)}
        else:
            dst, peer = route.at[outer + i], {"expert": inner_peer(q - outer + 2)}
        return pltpu.make_async_remote_copy(
            src_ref=route_send, dst_ref=dst, send_sem=route_ssem.at[q], recv_sem=route_rsem.at[q],
            device_id=peer, device_id_type=MESH)

    small = [pltpu.make_async_copy(a, b, t_sem.at[k]) for k, (a, b) in enumerate(
        ((slot_hbm, slot_ref), (ids_hbm, ids_ref), (gate_hbm, gate_ref)))]
    for c in small:
        c.start()
    for k in range(WINDOW):
        fetch(k // 3, k % 3)
    peers = outer + inner - 2
    barrier = pltpu.get_barrier_semaphore()
    for r in range(1, outer):
        pl.semaphore_signal(barrier, inc=1, device_id={"outer": outer_peer(r)}, device_id_type=MESH)
    for r in range(1, inner):
        pl.semaphore_signal(barrier, inc=1, device_id={"expert": inner_peer(r)}, device_id_type=MESH)

    for c in small:
        c.wait()
    slot = slot_ref[...]
    flat = jnp.where(slot >= 0, ids_ref[...] * cap + slot, -1).astype(F32)
    lanes = jnp.concatenate([flat, gate_ref[...]], axis=0)
    route_send[...] = lanes
    route[o] = lanes
    route[outer + i] = lanes
    pl.semaphore_wait(barrier, peers)
    for q in range(peers):
        copy_route(q).start()

    row = lax.broadcasted_iota(jnp.int32, (block, tokens), 0)
    row_in = o * block + row
    row_out = (row // span) * block + i * span + row % span

    def build_pick(k):
        want = jnp.where(k < outer, row_in, row_out).astype(F32)
        gates = jnp.zeros((block, tokens), F32)
        hits = jnp.zeros((block, tokens), F32)
        for j in range(top):
            hit = want == route[k, j:j + 1, :]
            gates = jnp.where(hit, route[k, top + j:top + j + 1, :], gates)
            hits = jnp.where(hit, 1.0, hits)
        used[k] = jnp.broadcast_to(jnp.max(hits, axis=1, keepdims=True), (block, tokens)).astype(BF16)
        g = gates.T
        high = jnp.minimum(g, BF16_MAX).astype(BF16)
        rest = g - high.astype(F32)
        mid = rest.astype(BF16)
        low = (rest - mid.astype(F32)).astype(BF16)
        pick[k, 0:tokens] = high
        pick[k, tokens:2 * tokens] = mid
        pick[k, 2 * tokens:3 * tokens] = low

    def expert_step(e, carry):
        s = lax.rem(e, SLOTS)
        arrived(e, 0)
        arrived(e, 1)
        x = x_buf[s].reshape(rows, width)
        tile = 256
        for n in range(ff // tile):
            cols = pl.ds(n * tile, tile)
            gate = jnp.dot(x, wg_buf[s, :, cols], preferred_element_type=F32)
            up = jnp.dot(x, wu_buf[s, :, cols], preferred_element_type=F32)
            h_buf[:, cols] = (gate * lax.logistic(gate) * up).astype(BF16)
        arrived(e, 2)
        h = h_buf[...]

        def down(*numbers):
            for n in numbers:
                y = jnp.dot(h, wd_buf[s, :, chunk_cols(n)], preferred_element_type=F32).astype(BF16)
                y_send[e, :, :, :, chunk_cols(n)] = y.reshape(outer, inner, cap, piece)

        down(0, 1)
        send_inner(e, 0)
        down(2)
        send_inner(e, 1)
        down(6, 7)
        send_inner(e, 2)
        down(4)
        send_outer(e)
        down(5, 3)
        send_half(e)
        y_in[:, i, e] = y_send[e, :, i, :, 0:split]
        y_out[:, o, e] = y_send[e, o, :, :, split:]
        y_half[:, seat, e] = y_send[e, o, :, :, mixed:split]

        @pl.when(e == 0)
        def _():
            for q in range(peers):
                copy_route(q).wait_recv()

        build_pick(e)
        return carry

    lax.fori_loop(0, local, expert_step, 0)

    for n in (LATER,) + MIXED:
        def send_last(e, carry):
            send_inner(e, n)
            return carry

        lax.fori_loop(0, local, send_last, 0)

    def partial_sum(k, slots, y):
        mask = jnp.concatenate([used[k, slots]] * (piece // tokens), axis=1) > 0
        y = jnp.where(mask, y, jnp.zeros((), BF16))
        s = jnp.dot(pick[k, :, slots], y, preferred_element_type=F32)
        return s[0:tokens] + s[tokens:2 * tokens] + s[2 * tokens:3 * tokens]

    def block_sum(n, k):
        return partial_sum(k, pl.ds(0, block), y_in[k, :, :, :, chunk_cols(n)].reshape(block, piece))

    def half_sum(n, k):
        y = y_half[k, :, :, :, pl.ds(n * piece - mixed, piece)].reshape(2 * span, piece)
        return partial_sum(outer + k, pl.ds(pl.multiple_of(half * 2 * span, 2 * span), 2 * span), y)

    def outer_sum(n, k):
        y = y_out[k, :, :, :, pl.ds(n * piece - split, piece)].reshape(block, piece)
        return partial_sum(outer + k, pl.ds(0, block), y)

    def sum_across(n):
        for r in range(1, inner):
            all_inner(n, r).wait_recv()
        for k in (1, 0):
            total = block_sum(n, across[k])

            @pl.when(middle == 1)
            def _():
                far[k, :, chunk_cols(n)] = total

            @pl.when(middle == 0)
            def _():
                z_send[1 + k, n] = total.astype(BF16)
                copy_across(n, k).start()

    def sum_near(n):
        z_send[0, n] = block_sum(n, near).astype(BF16)
        copy_near(n).start()

    def sum_inner(n, of):
        for r in range(1, inner):
            c_send[r - 1, n - MIXED[0]] = of(n, inner_peer(r)).astype(BF16)
            copy_c(n - MIXED[0], r).start()
        own[:, chunk_cols(n)] = of(n, i)

    def pass_on(n):
        @pl.when(middle == 1)
        def _():
            for k in (1, 0):
                copy_z(n, 1 + k, 2 + k, near).wait_recv()
                z_send[1 + k, n] = (far[k, :, chunk_cols(n)] + z_recv[2 + k, n].astype(F32)).astype(BF16)
                copy_across(n, k).start()

    def finish(n):
        total = own[:, chunk_cols(n)]
        if n < MIXED[0]:
            copy_z(n, 0, 0, near).wait_recv()
            total = total + z_recv[0, n].astype(F32)
        else:
            for r in range(1, inner):
                copy_c(n - MIXED[0], r).wait_recv()
                total = total + c_recv[r - 1, n - MIXED[0]].astype(F32)
        if n < INNER_CHUNKS:
            copy_z(n, 1, 1, near).wait_recv()
            total = total + z_recv[1, n].astype(F32)
        out_ref[:, chunk_cols(n)] = total.astype(BF16)

    for n in FIRST:
        sum_across(n)
    for r in range(1, outer):
        all_outer(r).wait_recv()
    all_half().wait_recv()
    for n in OUTER:
        sum_inner(n, outer_sum)
    for n in MIXED:
        sum_inner(n, half_sum)
    pass_on(0)
    sum_across(3)
    pass_on(1)
    sum_across(4)
    pass_on(2)
    sum_across(5)
    for n in FIRST + (LATER,):
        sum_near(n)
    pass_on(3)
    for n in FIRST + (LATER,):
        own[:, chunk_cols(n)] = block_sum(n, o)
    pass_on(4)
    pass_on(5)

    for q in range(peers):
        copy_route(q).wait_send()
    for r in range(1, inner):
        for n in range(INNER_CHUNKS):
            all_inner(n, r).wait_send()
    for r in range(1, outer):
        all_outer(r).wait_send()
    all_half().wait_send()
    for n in OUTER + MIXED:
        finish(n)
    for n in FIRST + (LATER,):
        finish(n)
    for n in OUTER + MIXED:
        for r in range(1, inner):
            copy_c(n - MIXED[0], r).wait_send()
    for n in range(INNER_CHUNKS):
        if n < MIXED[0]:
            copy_near(n).wait_send()
        for k in (1, 0):
            copy_across(n, k).wait_send()


def solution(mesh):
    outer = mesh.shape["outer"]
    inner = mesh.shape["expert"]

    def local_step(x_disp, w_gate, w_up, w_down, slot_idx, expert_ids, gate_wts):
        src, local, cap, width = x_disp.shape
        tokens, top = slot_idx.shape
        ff = w_gate.shape[2]
        block = inner * local * cap
        sources = outer + inner
        piece = width // CHUNKS
        split = INNER_CHUNKS * piece
        turned = CHUNKS - MIXED[0]
        peers = outer + inner - 2
        dma = pltpu.SemaphoreType.DMA
        hbm = pl.BlockSpec(memory_space=pltpu.HBM)
        vmem = pl.BlockSpec(memory_space=pltpu.VMEM)
        return pl.pallas_call(
            functools.partial(kernel, outer, inner),
            out_shape=jax.ShapeDtypeStruct((tokens, width), BF16),
            in_specs=[hbm] * 7,
            out_specs=vmem,
            scratch_shapes=[
                pltpu.VMEM((SLOTS, src, cap, width), BF16),
                pltpu.VMEM((SLOTS, width, ff), BF16),
                pltpu.VMEM((SLOTS, width, ff), BF16),
                pltpu.VMEM((SLOTS, ff, width), BF16),
                pltpu.VMEM((src * cap, ff), BF16),
                pltpu.VMEM((local, outer, inner, cap, width), BF16),
                pltpu.VMEM((outer, inner, local, cap, split), BF16),
                pltpu.VMEM((inner, outer, local, cap, width - split), BF16),
                pltpu.VMEM((inner, 2, local, cap, len(MIXED) * piece), BF16),
                pltpu.VMEM((top, tokens), jnp.int32),
                pltpu.VMEM((top, tokens), jnp.int32),
                pltpu.VMEM((top, tokens), F32),
                pltpu.VMEM((2 * top, tokens), F32),
                pltpu.VMEM((sources, 2 * top, tokens), F32),
                pltpu.VMEM((sources, 3 * tokens, block), BF16),
                pltpu.VMEM((sources, block, tokens), BF16),
                pltpu.VMEM((tokens, width), F32),
                pltpu.VMEM((2, tokens, split), F32),
                pltpu.VMEM((3, INNER_CHUNKS, tokens, piece), BF16),
                pltpu.VMEM((4, INNER_CHUNKS, tokens, piece), BF16),
                pltpu.VMEM((inner - 1, turned, tokens, piece), BF16),
                pltpu.VMEM((inner - 1, turned, tokens, piece), BF16),
                dma((4, SLOTS)), dma((3,)),
                dma((peers,)), dma((peers,)),
                dma((INNER_CHUNKS, inner - 1)), dma((INNER_CHUNKS, inner - 1)),
                dma((outer - 1,)), dma((outer - 1,)),
                dma, dma,
                dma((3, INNER_CHUNKS)), dma((4, INNER_CHUNKS)),
                dma((inner - 1, turned)), dma((inner - 1, turned)),
            ],
            compiler_params=pltpu.CompilerParams(
                collective_id=0, has_side_effects=True, vmem_limit_bytes=54_000_000),
        )(x_disp, w_gate, w_up, w_down, slot_idx.T, expert_ids.T, gate_wts.T)

    expert_spec = P(("outer", "expert"))
    token_spec = P(("data", "outer", "expert"))
    return jax.shard_map(local_step, mesh=mesh, in_specs=(P("data", ("outer", "expert")), expert_spec, expert_spec, expert_spec, token_spec, token_spec, token_spec), out_specs=token_spec, check_vma=False)
```

time: 63.7 us -> 59.7 us (0.937)
  Pallas kernels: 60.6 us -> 56.6 us
    pallas_call x1, Pallas kernels: 60.6 us -> 56.6 us  [local_step(): pl.pallas_call(functools.partial(kernel, outer, inner), out_shape=jax.Sha...]
where the time goes in v4:
time: 59.7 us; the launch traced here: 59.4 us
  Pallas kernels  56.6 us (95%)
  local copies, waits for them, and re-layouts  2.85 us (5%)
    pallas_call x1, Pallas kernels, local_step(): pl.pallas_call(functools.partial(kernel, outer, inner), out_shape=jax.Sha...  56.6 us
    unnamed x7, local copies, waits for them, and re-layouts  2.85 us

profile of v4, /device:TPU:0, one launch (start us, length us, event | category | flops | bytes accessed | tf_op | source)
XLA Modules:
  0.0 59.4 jit_solution(16594956431123291979)
XLA Ops:
  0.0 0.0 copy-start
  0.0 0.7 %copy-done = s32[128,8]{0,1:T(8,128)S(1)} copy-done((s32[128,8]{0,1:T(8,128)S(1)}, s32[128,8]{0,1:T(8,128)}, u32[]{:S(2)}) %copy-start) | copy-done | bytes 4120
  0.7 0.0 copy-start.1
  0.7 0.7 %copy-done.1 = s32[128,8]{0,1:T(8,128)S(1)} copy-done((s32[128,8]{0,1:T(8,128)S(1)}, s32[128,8]{0,1:T(8,128)}, u32[]{:S(2)}) %copy-start.1) | copy-done | bytes 4120
  1.4 0.0 copy-start.2
  1.4 0.7 %copy-done.2 = f32[128,8]{0,1:T(8,128)S(1)} copy-done((f32[128,8]{0,1:T(8,128)S(1)}, f32[128,8]{0,1:T(8,128)}, u32[]{:S(2)}) %copy-start.2) | copy-done | bytes 4120
  2.1 56.6 %shard_map.73 = bf16[128,2048]{1,0:T(8,128)(2,1)S(1)} custom-call(bf16[16,8,8,2048]{3,2,1,0:T(8,128)(2,1)} %x_hbm.1, bf16[8,2048,768]{2,1,0:T(8,128)(2,1)} %wg_hbm.1, bf16[8,2048,768]{2,1,0:T(8,128)(2,1)} %wu_hbm.1, bf16[8,768,2048]{2,1,0:T(8,128)(2,1)} %wd_hbm.1, s32[8,128]{1,0:T(8,128)S(1)} %bitcast.3, s32[8,128]{1,0:T(8,128)S(1)} %bitcast.4, ...), custom_call_target="tpu_custom_call" | custom-call | tf_op jit(solution)/shard_map/pallas_call | solution.py:372
  58.6 0.8 %copy.9 = bf16[128,2048]{1,0:T(8,128)(2,1)} copy(bf16[128,2048]{1,0:T(8,128)(2,1)S(1)} %shard_map.73) | data formatting | bytes 1048576
Async XLA Ops:
  0.0 0.7 %copy-start = (s32[128,8]{0,1:T(8,128)S(1)}, s32[128,8]{0,1:T(8,128)}, u32[]{:S(2)}) copy-start(s32[128,8]{0,1:T(8,128)} %param.11) | copy-start | bytes 12292
  0.7 0.7 %copy-start.1 = (s32[128,8]{0,1:T(8,128)S(1)}, s32[128,8]{0,1:T(8,128)}, u32[]{:S(2)}) copy-start(s32[128,8]{0,1:T(8,128)} %param.12) | copy-start | bytes 12292
  1.4 0.7 %copy-start.2 = (f32[128,8]{0,1:T(8,128)S(1)}, f32[128,8]{0,1:T(8,128)}, u32[]{:S(2)}) copy-start(f32[128,8]{0,1:T(8,128)} %param.13) | copy-start | bytes 12292

commit v5 on v4

--- a/solution.py
+++ b/solution.py
@@ -24,7 +24,7 @@
 
 
 def kernel(outer, inner, x_hbm, wg_hbm, wu_hbm, wd_hbm, slot_hbm, ids_hbm, gate_hbm, out_ref,
-           x_buf, wg_buf, wu_buf, wd_buf, h_buf, y_send, y_in, y_out, y_half, slot_ref, ids_ref, gate_ref, route_send, route, pick, used,
+           x_buf, wg_buf, wu_buf, wd_buf, h_buf, in_send, out_send, half_send, y_in, y_out, y_half, slot_ref, ids_ref, gate_ref, route_send, route, pick, used,
            own, far, z_send, z_recv, c_send, c_recv,
            w_sem, t_sem, route_ssem, route_rsem, i_ssem, i_rsem, r_ssem, r_rsem, h_ssem, h_rsem, z_ssem, z_rsem, c_ssem, c_rsem):
     src, local, cap, width = x_hbm.shape
@@ -85,28 +85,23 @@
 
     def send_inner(e, n):
         for r in range(1, inner):
-            inner_copy(y_send.at[e, blocks(n), inner_peer(r), :, chunk_cols(n)],
-                       y_in.at[blocks(n), i, e, :, chunk_cols(n)], n, r).start()
+            inner_copy(in_send.at[n, e, inner_peer(r), blocks(n)], y_in.at[n, i, e, blocks(n)], n, r).start()
 
     def all_inner(n, r):
-        return inner_copy(y_send.at[:, blocks(n), inner_peer(r), :, chunk_cols(n)],
-                          y_in.at[blocks(n), lax.rem(i + inner - r, inner), :, :, chunk_cols(n)], n, r)
+        return inner_copy(in_send.at[n, :, inner_peer(r), blocks(n)],
+                          y_in.at[n, lax.rem(i + inner - r, inner), :, blocks(n)], n, r)
 
     def outer_copy(src_ref, dst_ref, r):
         return pltpu.make_async_remote_copy(
             src_ref=src_ref, dst_ref=dst_ref, send_sem=r_ssem.at[r - 1], recv_sem=r_rsem.at[r - 1],
             device_id={"outer": outer_peer(r)}, device_id_type=MESH)
 
-    rest_cols = pl.ds(split, width - split)
-
     def send_outer(e):
         for r in range(1, outer):
-            outer_copy(y_send.at[e, outer_peer(r), :, :, rest_cols], y_out.at[:, o, e], r).start()
+            outer_copy(out_send.at[e, outer_peer(r)], y_out.at[o, e], r).start()
 
     def all_outer(r):
-        return outer_copy(y_send.at[:, outer_peer(r), :, :, rest_cols], y_out.at[:, lax.rem(o + outer - r, outer)], r)
-
-    half_cols = pl.ds(mixed, split - mixed)
+        return outer_copy(out_send.at[:, outer_peer(r)], y_out.at[lax.rem(o + outer - r, outer)], r)
 
     def half_copy(src_ref, dst_ref):
         return pltpu.make_async_remote_copy(
@@ -114,10 +109,10 @@
             device_id={"outer": near}, device_id_type=MESH)
 
     def send_half(e):
-        half_copy(y_send.at[e, near, :, :, half_cols], y_half.at[:, seat, e]).start()
+        half_copy(half_send.at[e, near - 2 * half], y_half.at[seat, e]).start()
 
     def all_half():
-        return half_copy(y_send.at[:, near, :, :, half_cols], y_half.at[:, 1 - seat])
+        return half_copy(half_send.at[:, near - 2 * half], y_half.at[1 - seat])
 
     def copy_z(p, q, slot, peer):
         return pltpu.make_async_remote_copy(
@@ -207,24 +202,37 @@
         arrived(e, 2)
         h = h_buf[...]
 
-        def down(*numbers):
-            for n in numbers:
-                y = jnp.dot(h, wd_buf[s, :, chunk_cols(n)], preferred_element_type=F32).astype(BF16)
-                y_send[e, :, :, :, chunk_cols(n)] = y.reshape(outer, inner, cap, piece)
-
-        down(0, 1)
-        send_inner(e, 0)
-        down(2)
-        send_inner(e, 1)
-        down(6, 7)
-        send_inner(e, 2)
-        down(4)
+        def down(n):
+            y = jnp.dot(h, wd_buf[s, :, chunk_cols(n)], preferred_element_type=F32).astype(BF16)
+            return y.reshape(outer, inner, cap, piece)
+
+        for n in OUTER:
+            out_send[e, :, :, :, pl.ds((n - OUTER[0]) * piece, piece)] = down(n)
+        for n in MIXED:
+            y = down(n)
+            for k in range(inner):
+                in_send[n, e, k] = y[:, k]
+            cols = pl.ds((n - MIXED[0]) * piece, piece)
+
+            @pl.when(half == 0)
+            def _():
+                half_send[e, :, :, :, cols] = y[0:2]
+
+            @pl.when(half == 1)
+            def _():
+                half_send[e, :, :, :, cols] = y[2:4]
         send_outer(e)
-        down(5, 3)
-        send_half(e)
-        y_in[:, i, e] = y_send[e, :, i, :, 0:split]
-        y_out[:, o, e] = y_send[e, o, :, :, split:]
-        y_half[:, seat, e] = y_send[e, o, :, :, mixed:split]
+        for n in FIRST + (LATER,):
+            y = down(n)
+            for k in range(inner):
+                in_send[n, e, k] = y[:, k]
+            if n == FIRST[0]:
+                send_half(e)
+            else:
+                send_inner(e, n - 1)
+        y_in[:, i, e] = in_send[:, e, i]
+        y_out[o, e] = out_send[e, o]
+        y_half[seat, e] = half_send[e, seat]
 
         @pl.when(e == 0)
         def _():
@@ -250,14 +258,14 @@
         return s[0:tokens] + s[tokens:2 * tokens] + s[2 * tokens:3 * tokens]
 
     def block_sum(n, k):
-        return partial_sum(k, pl.ds(0, block), y_in[k, :, :, :, chunk_cols(n)].reshape(block, piece))
+        return partial_sum(k, pl.ds(0, block), y_in[n, :, :, k].reshape(block, piece))
 
     def half_sum(n, k):
-        y = y_half[k, :, :, :, pl.ds(n * piece - mixed, piece)].reshape(2 * span, piece)
+        y = y_half[:, :, k, :, pl.ds(n * piece - mixed, piece)].reshape(2 * span, piece)
         return partial_sum(outer + k, pl.ds(pl.multiple_of(half * 2 * span, 2 * span), 2 * span), y)
 
     def outer_sum(n, k):
-        y = y_out[k, :, :, :, pl.ds(n * piece - split, piece)].reshape(block, piece)
+        y = y_out[:, :, k, :, pl.ds(n * piece - split, piece)].reshape(block, piece)
         return partial_sum(outer + k, pl.ds(0, block), y)
 
     def sum_across(n):
@@ -380,10 +388,12 @@
                 pltpu.VMEM((SLOTS, width, ff), BF16),
                 pltpu.VMEM((SLOTS, ff, width), BF16),
                 pltpu.VMEM((src * cap, ff), BF16),
-                pltpu.VMEM((local, outer, inner, cap, width), BF16),
-                pltpu.VMEM((outer, inner, local, cap, split), BF16),
-                pltpu.VMEM((inner, outer, local, cap, width - split), BF16),
-                pltpu.VMEM((inner, 2, local, cap, len(MIXED) * piece), BF16),
+                pltpu.VMEM((INNER_CHUNKS, local, inner, outer, cap, piece), BF16),
+                pltpu.VMEM((local, outer, inner, cap, width - split), BF16),
+                pltpu.VMEM((local, 2, inner, cap, len(MIXED) * piece), BF16),
+                pltpu.VMEM((INNER_CHUNKS, inner, local, outer, cap, piece), BF16),
+                pltpu.VMEM((outer, local, inner, cap, width - split), BF16),
+                pltpu.VMEM((2, local, inner, cap, len(MIXED) * piece), BF16),
                 pltpu.VMEM((top, tokens), jnp.int32),
                 pltpu.VMEM((top, tokens), jnp.int32),
                 pltpu.VMEM((top, tokens), F32),
@@ -407,7 +417,7 @@
             ],
             compiler_params=pltpu.CompilerParams(
                 collective_id=0, has_side_effects=True, vmem_limit_bytes=54_000_000),
-        )(x_disp, w_gate, w_up, w_down, slot_idx.T, expert_ids.T, gate_wts.T)
+        )(x_disp, w_gate, w_up, w_down, *(pltpu.with_memory_space_constraint(a.T, pltpu.HBM) for a in (slot_idx, expert_ids, gate_wts)))
 
     expert_spec = P(("outer", "expert"))
     token_spec = P(("data", "outer", "expert"))

time: 59.7 us -> 61.5 us (1.030)
  Pallas kernels: 56.6 us -> 60.6 us
  local copies, waits for them, and re-layouts: 2.85 us -> 0.8 us
    pallas_call x1, Pallas kernels: 56.6 us -> 60.6 us  [local_step(): pl.pallas_call(functools.partial(kernel, outer, inner), out_shape=jax.Sha...]
    unnamed x7 -> x1, local copies, waits for them, and re-layouts: 2.85 us -> 0.8 us
where the time goes in v5:
time: 61.5 us; the launch traced here: 61.4 us
  Pallas kernels  60.6 us (99%)
  local copies, waits for them, and re-layouts  0.8 us (1%)
    pallas_call x1, Pallas kernels, local_step(): pl.pallas_call(functools.partial(kernel, outer, inner), out_shape=jax.Sha...  60.6 us

profile of v5, /device:TPU:0, one launch (start us, length us, event | category | flops | bytes accessed | tf_op | source)
XLA Modules:
  0.0 61.4 jit_solution(4251173751419017010)
XLA Ops:
  0.0 60.6 %shard_map.73 = bf16[128,2048]{1,0:T(8,128)(2,1)S(1)} custom-call(bf16[16,8,8,2048]{3,2,1,0:T(8,128)(2,1)} %x_hbm.1, bf16[8,2048,768]{2,1,0:T(8,128)(2,1)} %wg_hbm.1, bf16[8,2048,768]{2,1,0:T(8,128)(2,1)} %wu_hbm.1, bf16[8,768,2048]{2,1,0:T(8,128)(2,1)} %wd_hbm.1, s32[8,128]{1,0:T(8,128)} %bitcast.3, s32[8,128]{1,0:T(8,128)} %bitcast.4, f32[8,128]{1,0:T(8,128)} %bitcast.5), custom_call_target="tpu_custom_call" | custom-call | tf_op jit(solution)/shard_map/pallas_call | solution.py:380
  60.6 0.8 %copy.9 = bf16[128,2048]{1,0:T(8,128)(2,1)} copy(bf16[128,2048]{1,0:T(8,128)(2,1)S(1)} %shard_map.73) | data formatting | bytes 1048576

commit v6 on v4

--- a/solution.py
+++ b/solution.py
@@ -407,7 +407,7 @@
             ],
             compiler_params=pltpu.CompilerParams(
                 collective_id=0, has_side_effects=True, vmem_limit_bytes=54_000_000),
-        )(x_disp, w_gate, w_up, w_down, slot_idx.T, expert_ids.T, gate_wts.T)
+        )(x_disp, w_gate, w_up, w_down, *(pltpu.with_memory_space_constraint(a.T, pltpu.HBM) for a in (slot_idx, expert_ids, gate_wts)))
 
     expert_spec = P(("outer", "expert"))
     token_spec = P(("data", "outer", "expert"))

time: 59.7 us -> 59.2 us (level)
  local copies, waits for them, and re-layouts: 2.85 us -> 0.8 us
  Pallas kernels: 56.6 us -> 58.3 us
    unnamed x7 -> x1, local copies, waits for them, and re-layouts: 2.85 us -> 0.8 us
    pallas_call x1, Pallas kernels: 56.6 us -> 58.3 us  [local_step(): pl.pallas_call(functools.partial(kernel, outer, inner), out_shape=jax.Sha...]
where the time goes in v6:
time: 59.2 us; the launch traced here: 59.1 us
  Pallas kernels  58.3 us (98%)
  local copies, waits for them, and re-layouts  0.8 us (1%)
    pallas_call x1, Pallas kernels, local_step(): pl.pallas_call(functools.partial(kernel, outer, inner), out_shape=jax.Sha...  58.3 us

profile of v6, /device:TPU:0, one launch (start us, length us, event | category | flops | bytes accessed | tf_op | source)
XLA Modules:
  0.0 59.1 jit_solution(9912517254886237023)
XLA Ops:
  0.0 58.3 %shard_map.73 = bf16[128,2048]{1,0:T(8,128)(2,1)S(1)} custom-call(bf16[16,8,8,2048]{3,2,1,0:T(8,128)(2,1)} %x_hbm.1, bf16[8,2048,768]{2,1,0:T(8,128)(2,1)} %wg_hbm.1, bf16[8,2048,768]{2,1,0:T(8,128)(2,1)} %wu_hbm.1, bf16[8,768,2048]{2,1,0:T(8,128)(2,1)} %wd_hbm.1, s32[8,128]{1,0:T(8,128)} %bitcast.3, s32[8,128]{1,0:T(8,128)} %bitcast.4, f32[8,128]{1,0:T(8,128)} %bitcast.5), custom_call_target="tpu_custom_call" | custom-call | tf_op jit(solution)/shard_map/pallas_call | solution.py:372
  58.3 0.8 %copy.9 = bf16[128,2048]{1,0:T(8,128)(2,1)} copy(bf16[128,2048]{1,0:T(8,128)(2,1)S(1)} %shard_map.73) | data formatting | bytes 1048576
